TPU v7x, 128 devices: a whole 4x4x4 slice. The times are simulated.
128 devices in a mesh: lon: 32 (over z, y_lo, x), ch: 4 (over y_hi, core).
Axes of the slice: x: 4, y: 4 (y_hi: 2, y_lo: 2; y = y_hi * 2 + y_lo), z: 4, core: 2. Of those that a mesh axis runs over, the one named last changes fastest.
Arguments:
- grid_inputs: bfloat16 [921600, 474], P('lon'), may hold values from -6 to 6
- embed_weight: bfloat16 [474, 512], replicated, may hold values from -0.25 to 0.25
- embed_bias: float32 [512], replicated, may hold values from -3 to 3
- mesh_latent: bfloat16 [20480, 512], P('lon', 'ch'), may hold values from -6 to 6
- edge_features: bfloat16 [4, 720896], P(None, 'lon'), may hold values from -6 to 6
- senders: int32 [720896], P('lon'), may hold values from 0 to 921599, as said below
- receivers: int32 [720896], P('lon'), may hold values from 0 to 20479, as said below
- sender_weight: bfloat16 [512, 512], P(None, 'ch'), may hold values from -0.25 to 0.25
- receiver_weight: bfloat16 [512, 512], P(None, 'ch'), may hold values from -0.25 to 0.25
- feature_weight: bfloat16 [4, 512], P(None, 'ch'), may hold values from -3 to 3
- hidden_bias: float32 [512], P('ch'), may hold values from -3 to 3
- message_weight: bfloat16 [512, 512], P('ch'), may hold values from -0.25 to 0.25
- message_bias: float32 [512], replicated, may hold values from -1.2 to 1.2
- norm_gain: float32 [512], P('ch'), may hold values from 0.5 to 1.5
- norm_shift: float32 [512], P('ch'), may hold values from -3 to 3
Outputs:
- mesh_out: bfloat16 [20480, 512], P('lon', 'ch')
Inputs may be any that keep to these rules, and one draw needn't show every extreme that they name: Edge e belongs to block b = e // 22528. Its sender is c * 640 + t with latitude row t and a column c that lies, counted around the closed circle of 1440 columns, at most 4 columns before or after the block's own columns b * 45 to b * 45 + 44; some block reaches 4 columns on both sides. Within each aligned run of min(2048, 22528) edges of a block, the senders' columns, counted from the block's first widened column, lie within 7 consecutive columns. `receivers`: the receiver of edge e lies among the mesh nodes b * 640 to b * 640 + 639 of its block b = e // 22528; a mesh node may receive no edge.
All inputs are finite; a program needn't handle non-finite values.
Results may differ from a plain program's by a relative error of at most 0.0028.
Values may be sent and summed in bfloat16 or wider, within the bound.
No kernel may reach another device: no remote copies, remote signals or barrier semaphores. Data moves between devices by JAX's collectives and lax.ppermute only.
A program may use at most 128 MiB of HBM per device.

v0:
```python
import jax
import jax.numpy as jnp
from jax import lax
from jax.sharding import PartitionSpec as P

LAT = 640
HALO = 4


def with_halo(block, sides, width):
    for axis, dim in sides:
        count = lax.axis_size(axis)
        forward = [(i, i + 1) for i in range(count - 1)]
        forward.append((count - 1, 0))
        backward = [(target, source) for source, target in forward]
        low = lax.ppermute(
            lax.slice_in_dim(block, block.shape[dim] - width, None, axis=dim), axis, forward
        )
        high = lax.ppermute(lax.slice_in_dim(block, 0, width, axis=dim), axis, backward)
        block = jnp.concatenate([low, block, high], axis=dim)
    return block


def split_up(value, dim, devices):
    before, after = (value.shape[:dim], value.shape[dim + 1 :])
    return jnp.moveaxis(value.reshape(*before, devices, -1, *after), dim, 0)


def sent_and_summed(value, axis, dim):
    devices = lax.axis_size(axis)
    parts = lax.all_to_all(split_up(value, dim, devices), axis, 0, 0, tiled=True)
    return jnp.sum(parts, axis=0)


def embedded(grid_rows, embed_weight, embed_bias):
    return jax.nn.silu(
        jnp.dot(grid_rows, embed_weight, preferred_element_type=jnp.float32) + embed_bias
    ).astype(jnp.bfloat16)


def on_device(
    grid_inputs,
    embed_weight,
    embed_bias,
    mesh_latent,
    edge_features,
    senders,
    receivers,
    sender_weight,
    receiver_weight,
    feature_weight,
    hidden_bias,
    message_weight,
    message_bias,
    norm_gain,
    norm_shift,
):
    lon_count = lax.axis_size("lon")
    lon_place = lax.axis_index("lon")
    ch_place = lax.axis_index("ch")
    columns = grid_inputs.shape[0] // LAT
    mesh_nodes = mesh_latent.shape[0]
    share_width = mesh_latent.shape[1]
    full_width = message_weight.shape[1]
    latent = embedded(grid_inputs, embed_weight, embed_bias)
    own_terms = jnp.dot(latent, sender_weight, preferred_element_type=jnp.float32)
    widened = with_halo(
        own_terms.reshape(columns, LAT, share_width).astype(jnp.bfloat16), (("lon", 0),), HALO
    ).astype(jnp.float32)
    sent_terms = widened.reshape(-1, share_width)
    grid_column = senders // LAT
    shifted = jnp.mod(grid_column - lon_place * columns + HALO, columns * lon_count)
    local_send = shifted * LAT + senders % LAT
    local_recv = receivers - lon_place * mesh_nodes
    full_mesh = lax.all_gather(mesh_latent, "ch", axis=1, tiled=True)
    recv_terms = jnp.dot(full_mesh, receiver_weight, preferred_element_type=jnp.float32)
    edge_count = senders.shape[0]
    block_rows = min(2048, edge_count)
    steps_count = edge_count // block_rows
    feature_blocks = jnp.transpose(
        edge_features.reshape(edge_features.shape[0], steps_count, block_rows), (1, 0, 2)
    )
    node_ids = lax.broadcasted_iota(jnp.int32, (1, mesh_nodes), 1)

    def accumulate(carried, pieces):
        totals, tallies = carried
        send_ids, recv_ids, features = pieces
        before = jnp.take(sent_terms, send_ids, axis=0) + jnp.take(recv_terms, recv_ids, axis=0)
        before = (
            before
            + lax.dot_general(
                features,
                feature_weight,
                (((0,), (0,)), ((), ())),
                preferred_element_type=jnp.float32,
            )
            + hidden_bias
        )
        hidden = jax.nn.silu(before).astype(jnp.bfloat16)
        one_hot = (recv_ids[:, None] == node_ids).astype(jnp.bfloat16)
        totals = totals + lax.dot_general(
            one_hot, hidden, (((0,), (0,)), ((), ())), preferred_element_type=jnp.float32
        )
        tallies = tallies + jnp.sum(one_hot, axis=0, dtype=jnp.float32)
        return ((totals, tallies), None)

    start = (
        jnp.zeros((mesh_nodes, share_width), jnp.float32),
        jnp.zeros((mesh_nodes,), jnp.float32),
    )
    pieces_all = (
        local_send.reshape(steps_count, block_rows),
        local_recv.reshape(steps_count, block_rows),
        feature_blocks,
    )
    (totals, tallies), ignored = lax.scan(accumulate, start, pieces_all)
    partial_value = jnp.dot(
        totals, message_weight.astype(jnp.float32), precision=lax.Precision.HIGHEST
    )
    bias_share = lax.dynamic_slice_in_dim(message_bias, ch_place * share_width, share_width, 0)
    node_share = sent_and_summed(partial_value, "ch", 1) + tallies[:, None] * bias_share
    first_sum, second = lax.psum(
        (
            jnp.sum(node_share, axis=1, keepdims=True),
            jnp.sum(jnp.square(node_share), axis=1, keepdims=True),
        ),
        "ch",
    )
    centre = first_sum / full_width
    spread = second / full_width - jnp.square(centre)
    normed = (node_share - centre) * lax.rsqrt(spread + 1.0)
    return (mesh_latent.astype(jnp.float32) + normed * norm_gain + norm_shift).astype(jnp.bfloat16)


def solution(mesh):
    return jax.shard_map(
        on_device,
        mesh=mesh,
        in_specs=(
            P("lon", None),
            P(),
            P(),
            P("lon", "ch"),
            P(None, "lon"),
            P("lon"),
            P("lon"),
            P(None, "ch"),
            P(None, "ch"),
            P(None, "ch"),
            P("ch"),
            P("ch", None),
            P(),
            P("ch"),
            P("ch"),
        ),
        out_specs=P("lon", "ch"),
        check_vma=False,
    )
```

profile of v0, /device:TPU:6, one launch (start us, length us, event | category | flops | bytes accessed | tf_op | source)
XLA Modules:
  0.0 351.8 jit_solution(3035467392577934759)
XLA Ops:
  0.0 1.0 copy-done
  1.0 31.8 %multiply_convert_fusion.1 = bf16[28800,512]{1,0:T(8,128)(2,1)} fusion(bf16[28800,474]{0,1:T(8,128)(2,1)} %param.17, bf16[474,512]{1,0:T(8,128)(2,1)S(1)} %copy-done, f32[512]{0:T(512)} %param.19), kind=kOutput, calls=%fused_computation.33 | convolution fusion | flops 14067302400 | bytes 57281024 | tf_op jit(solution)/shard_map/dot_general | solution.py:37
  32.8 13.5 %convolution_convert_fusion = bf16[28800,128]{1,0:T(8,128)(2,1)S(1)} fusion(bf16[28800,512]{1,0:T(8,128)(2,1)} %multiply_convert_fusion.1, bf16[512,128]{1,0:T(8,128)(2,1)S(1)} %copy-done.4), kind=kOutput, calls=%fused_computation.34 | convolution fusion | flops 3778560000 | bytes 36995072 | tf_op jit(solution)/shard_map/dot_general | solution.py:66
  46.3 2.9 copy-done.2
  49.3 1.2 fusion.27
  50.5 1.5 collective-permute-start
  51.9 0.5 collective-permute-start.1
  52.5 0.2 fusion.25
  52.8 23.7 %all_gather.3 = bf16[640,512]{1,0:T(8,128)(2,1)S(1)} all-gather(bf16[640,128]{1,0:T(8,128)(2,1)S(1)} %copy-done.3), channel_id=1, replica_groups=mesh['lon'=32,'ch'=4] {'ch'}, dimensions={1}, use_global_device_ids=true | all-gather | bytes 819200 | tf_op jit(solution)/shard_map/all_gather | solution.py:75
  76.4 0.3 fusion.28
  76.8 4.3 %pad_maximum_fusion = bf16[53,640,128]{2,1,0:T(8,128)(2,1)S(1)} fusion(bf16[4,640,128]{2,1,0:T(8,128)(2,1)S(1)} %collective-permute-done.1, bf16[45,640,128]{2,1,0:T(8,128)(2,1)} %bitcast.47, bf16[4,640,128]{2,1,0:T(8,128)(2,1)S(1)} %collective-permute-done), kind=kLoop, calls=%fused_computation.35 | loop fusion | flops 8683520 | bytes 17367040 | tf_op jit(solution)/shard_map/concatenate | solution.py:20
  81.1 6.2 %bitcast_convert_fusion = f32[33920,128]{1,0:T(8,128)} fusion(bf16[53,640,128]{2,1,0:T(8,128)(2,1)S(1)} %pad_maximum_fusion), kind=kLoop, calls=%fused_computation.36 | loop fusion | flops 4341760 | bytes 26050560 | tf_op jit(solution)/shard_map/convert_element_type | solution.py:69
  87.3 231.8 %while.13 = (s32[]{:T(128)}, f32[640,128]{1,0:T(8,128)S(1)}, f32[640]{0:T(1024)S(1)}, s32[11,2048]{1,0:T(8,128)S(1)}, s32[11,2048]{1,0:T(8,128)S(1)}, /*index=5*...) while((s32[]{:T(128)}, f32[640,128]{1,0:T(8,128)S(1)}, ...), condition=%wide.region_2.3_spmd.clone, body=%wide.region_0.2_spmd.clone.sunk | while | flops 347021952 | bytes 7114884 | solution.py:116
  87.4 5.5 %gather_fusion = f32[2048,128]{1,0:T(8,128)S(1)} fusion(f32[640,128]{1,0:T(8,128)S(1)} %get-tuple-element.233, s32[2048]{0:T(1024)S(1)} %broadcast_clamp_fusion.4), kind=kCustom, calls=%fused_computation.1.clone.clone.1 | custom fusion | bytes 2105344 | tf_op jit(solution)/shard_map/while/body/eval_jaxpr/jit(_take)/gather | solution.py:88
  92.9 11.4 %gather_fusion.1 = f32[2048,128]{1,0:T(8,128)S(1)} fusion(f32[33920,128]{1,0:T(8,128)} %get-tuple-element.232, s32[2048]{0:T(1024)S(1)} %broadcast_clamp_fusion.5), kind=kCustom, calls=%fused_computation.clone.clone.1 | custom fusion | bytes 2105344 | tf_op jit(solution)/shard_map/while/body/eval_jaxpr/jit(_take)/gather | solution.py:88
  104.3 3.4 fusion.44
  107.7 0.7 convert_reduce_fusion.2
  108.4 5.5 %gather_fusion = f32[2048,128]{1,0:T(8,128)S(1)} fusion(f32[640,128]{1,0:T(8,128)S(1)} %get-tuple-element.233, s32[2048]{0:T(1024)S(1)} %broadcast_clamp_fusion.4), kind=kCustom, calls=%fused_computation.1.clone.clone.1 | custom fusion | bytes 2105344 | tf_op jit(solution)/shard_map/while/body/eval_jaxpr/jit(_take)/gather | solution.py:88
  113.9 11.4 %gather_fusion.1 = f32[2048,128]{1,0:T(8,128)S(1)} fusion(f32[33920,128]{1,0:T(8,128)} %get-tuple-element.232, s32[2048]{0:T(1024)S(1)} %broadcast_clamp_fusion.5), kind=kCustom, calls=%fused_computation.clone.clone.1 | custom fusion | bytes 2105344 | tf_op jit(solution)/shard_map/while/body/eval_jaxpr/jit(_take)/gather | solution.py:88
  125.4 3.4 fusion.44
  128.7 0.7 convert_reduce_fusion.2
  129.5 5.5 %gather_fusion = f32[2048,128]{1,0:T(8,128)S(1)} fusion(f32[640,128]{1,0:T(8,128)S(1)} %get-tuple-element.233, s32[2048]{0:T(1024)S(1)} %broadcast_clamp_fusion.4), kind=kCustom, calls=%fused_computation.1.clone.clone.1 | custom fusion | bytes 2105344 | tf_op jit(solution)/shard_map/while/body/eval_jaxpr/jit(_take)/gather | solution.py:88
  135.0 11.4 %gather_fusion.1 = f32[2048,128]{1,0:T(8,128)S(1)} fusion(f32[33920,128]{1,0:T(8,128)} %get-tuple-element.232, s32[2048]{0:T(1024)S(1)} %broadcast_clamp_fusion.5), kind=kCustom, calls=%fused_computation.clone.clone.1 | custom fusion | bytes 2105344 | tf_op jit(solution)/shard_map/while/body/eval_jaxpr/jit(_take)/gather | solution.py:88
  146.4 3.4 fusion.44
  149.8 0.7 convert_reduce_fusion.2
  150.6 5.5 %gather_fusion = f32[2048,128]{1,0:T(8,128)S(1)} fusion(f32[640,128]{1,0:T(8,128)S(1)} %get-tuple-element.233, s32[2048]{0:T(1024)S(1)} %broadcast_clamp_fusion.4), kind=kCustom, calls=%fused_computation.1.clone.clone.1 | custom fusion | bytes 2105344 | tf_op jit(solution)/shard_map/while/body/eval_jaxpr/jit(_take)/gather | solution.py:88
  156.1 11.4 %gather_fusion.1 = f32[2048,128]{1,0:T(8,128)S(1)} fusion(f32[33920,128]{1,0:T(8,128)} %get-tuple-element.232, s32[2048]{0:T(1024)S(1)} %broadcast_clamp_fusion.5), kind=kCustom, calls=%fused_computation.clone.clone.1 | custom fusion | bytes 2105344 | tf_op jit(solution)/shard_map/while/body/eval_jaxpr/jit(_take)/gather | solution.py:88
  167.5 3.4 fusion.44
  170.9 0.7 convert_reduce_fusion.2
  171.7 5.5 %gather_fusion = f32[2048,128]{1,0:T(8,128)S(1)} fusion(f32[640,128]{1,0:T(8,128)S(1)} %get-tuple-element.233, s32[2048]{0:T(1024)S(1)} %broadcast_clamp_fusion.4), kind=kCustom, calls=%fused_computation.1.clone.clone.1 | custom fusion | bytes 2105344 | tf_op jit(solution)/shard_map/while/body/eval_jaxpr/jit(_take)/gather | solution.py:88
  177.1 11.4 %gather_fusion.1 = f32[2048,128]{1,0:T(8,128)S(1)} fusion(f32[33920,128]{1,0:T(8,128)} %get-tuple-element.232, s32[2048]{0:T(1024)S(1)} %broadcast_clamp_fusion.5), kind=kCustom, calls=%fused_computation.clone.clone.1 | custom fusion | bytes 2105344 | tf_op jit(solution)/shard_map/while/body/eval_jaxpr/jit(_take)/gather | solution.py:88
  188.6 3.4 fusion.44
  192.0 0.7 convert_reduce_fusion.2
  192.7 5.5 %gather_fusion = f32[2048,128]{1,0:T(8,128)S(1)} fusion(f32[640,128]{1,0:T(8,128)S(1)} %get-tuple-element.233, s32[2048]{0:T(1024)S(1)} %broadcast_clamp_fusion.4), kind=kCustom, calls=%fused_computation.1.clone.clone.1 | custom fusion | bytes 2105344 | tf_op jit(solution)/shard_map/while/body/eval_jaxpr/jit(_take)/gather | solution.py:88
  198.2 11.4 %gather_fusion.1 = f32[2048,128]{1,0:T(8,128)S(1)} fusion(f32[33920,128]{1,0:T(8,128)} %get-tuple-element.232, s32[2048]{0:T(1024)S(1)} %broadcast_clamp_fusion.5), kind=kCustom, calls=%fused_computation.clone.clone.1 | custom fusion | bytes 2105344 | tf_op jit(solution)/shard_map/while/body/eval_jaxpr/jit(_take)/gather | solution.py:88
  209.6 3.4 fusion.44
  213.0 0.7 convert_reduce_fusion.2
  213.8 5.5 %gather_fusion = f32[2048,128]{1,0:T(8,128)S(1)} fusion(f32[640,128]{1,0:T(8,128)S(1)} %get-tuple-element.233, s32[2048]{0:T(1024)S(1)} %broadcast_clamp_fusion.4), kind=kCustom, calls=%fused_computation.1.clone.clone.1 | custom fusion | bytes 2105344 | tf_op jit(solution)/shard_map/while/body/eval_jaxpr/jit(_take)/gather | solution.py:88
  219.3 11.4 %gather_fusion.1 = f32[2048,128]{1,0:T(8,128)S(1)} fusion(f32[33920,128]{1,0:T(8,128)} %get-tuple-element.232, s32[2048]{0:T(1024)S(1)} %broadcast_clamp_fusion.5), kind=kCustom, calls=%fused_computation.clone.clone.1 | custom fusion | bytes 2105344 | tf_op jit(solution)/shard_map/while/body/eval_jaxpr/jit(_take)/gather | solution.py:88
  230.7 3.4 fusion.44
  234.1 0.7 convert_reduce_fusion.2
  234.9 5.5 %gather_fusion = f32[2048,128]{1,0:T(8,128)S(1)} fusion(f32[640,128]{1,0:T(8,128)S(1)} %get-tuple-element.233, s32[2048]{0:T(1024)S(1)} %broadcast_clamp_fusion.4), kind=kCustom, calls=%fused_computation.1.clone.clone.1 | custom fusion | bytes 2105344 | tf_op jit(solution)/shard_map/while/body/eval_jaxpr/jit(_take)/gather | solution.py:88
  240.4 11.4 %gather_fusion.1 = f32[2048,128]{1,0:T(8,128)S(1)} fusion(f32[33920,128]{1,0:T(8,128)} %get-tuple-element.232, s32[2048]{0:T(1024)S(1)} %broadcast_clamp_fusion.5), kind=kCustom, calls=%fused_computation.clone.clone.1 | custom fusion | bytes 2105344 | tf_op jit(solution)/shard_map/while/body/eval_jaxpr/jit(_take)/gather | solution.py:88
  251.8 3.4 fusion.44
  255.2 0.7 convert_reduce_fusion.2
  256.0 5.5 %gather_fusion = f32[2048,128]{1,0:T(8,128)S(1)} fusion(f32[640,128]{1,0:T(8,128)S(1)} %get-tuple-element.233, s32[2048]{0:T(1024)S(1)} %broadcast_clamp_fusion.4), kind=kCustom, calls=%fused_computation.1.clone.clone.1 | custom fusion | bytes 2105344 | tf_op jit(solution)/shard_map/while/body/eval_jaxpr/jit(_take)/gather | solution.py:88
  261.4 11.4 %gather_fusion.1 = f32[2048,128]{1,0:T(8,128)S(1)} fusion(f32[33920,128]{1,0:T(8,128)} %get-tuple-element.232, s32[2048]{0:T(1024)S(1)} %broadcast_clamp_fusion.5), kind=kCustom, calls=%fused_computation.clone.clone.1 | custom fusion | bytes 2105344 | tf_op jit(solution)/shard_map/while/body/eval_jaxpr/jit(_take)/gather | solution.py:88
  272.9 3.4 fusion.44
  276.2 0.7 convert_reduce_fusion.2
  277.0 5.5 %gather_fusion = f32[2048,128]{1,0:T(8,128)S(1)} fusion(f32[640,128]{1,0:T(8,128)S(1)} %get-tuple-element.233, s32[2048]{0:T(1024)S(1)} %broadcast_clamp_fusion.4), kind=kCustom, calls=%fused_computation.1.clone.clone.1 | custom fusion | bytes 2105344 | tf_op jit(solution)/shard_map/while/body/eval_jaxpr/jit(_take)/gather | solution.py:88
  282.5 11.4 %gather_fusion.1 = f32[2048,128]{1,0:T(8,128)S(1)} fusion(f32[33920,128]{1,0:T(8,128)} %get-tuple-element.232, s32[2048]{0:T(1024)S(1)} %broadcast_clamp_fusion.5), kind=kCustom, calls=%fused_computation.clone.clone.1 | custom fusion | bytes 2105344 | tf_op jit(solution)/shard_map/while/body/eval_jaxpr/jit(_take)/gather | solution.py:88
  293.9 3.4 fusion.44
  297.3 0.7 convert_reduce_fusion.2
  298.1 5.5 %gather_fusion = f32[2048,128]{1,0:T(8,128)S(1)} fusion(f32[640,128]{1,0:T(8,128)S(1)} %get-tuple-element.233, s32[2048]{0:T(1024)S(1)} %broadcast_clamp_fusion.4), kind=kCustom, calls=%fused_computation.1.clone.clone.1 | custom fusion | bytes 2105344 | tf_op jit(solution)/shard_map/while/body/eval_jaxpr/jit(_take)/gather | solution.py:88
  303.6 11.4 %gather_fusion.1 = f32[2048,128]{1,0:T(8,128)S(1)} fusion(f32[33920,128]{1,0:T(8,128)} %get-tuple-element.232, s32[2048]{0:T(1024)S(1)} %broadcast_clamp_fusion.5), kind=kCustom, calls=%fused_computation.clone.clone.1 | custom fusion | bytes 2105344 | tf_op jit(solution)/shard_map/while/body/eval_jaxpr/jit(_take)/gather | solution.py:88
  315.0 3.4 fusion.44
  318.4 0.7 convert_reduce_fusion.2
  319.1 1.8 fusion.29
  320.9 3.5 %all-to-all-start = ((f32[4,640,128]{1,2,0:T(8,128)}), f32[4,640,128]{1,2,0:T(8,128)S(1)}, u32[]{:S(2)}, u32[]{:S(2)}) async-start(f32[4,640,128]{1,2,0:T(8,128)} %bitcast.7), calls=%async_computation | async-start | bytes 2621440 | tf_op jit(solution)/shard_map/all_to_all | solution.py:31
  324.6 0.8 dynamic_slice.14
  325.4 17.8 %all-to-all-done = f32[4,640,128]{1,2,0:T(8,128)S(1)} async-done(((f32[4,640,128]{1,2,0:T(8,128)}), f32[4,640,128]{1,2,0:T(8,128)S(1)}, u32[]{:S(2)}, u32[]{:S(2)}) %all-to-all-start) | async-done | bytes 1310752 | tf_op jit(solution)/shard_map/all_to_all | solution.py:31
  343.4 7.4 %all-reduce = (f32[640,1]{0,1:T(1,128)S(1)}, f32[640,1]{0,1:T(1,128)S(1)}) all-reduce(f32[640,1]{0,1:T(1,128)S(1)} %broadcast_in_dim.39, f32[640,1]{0,1:T(1,128)S(1)} %broadcast_in_dim.40), channel_id=1, replica_groups=mesh['lon'=32,'ch'=4] {'ch'}, use_global_device_ids=true, to_apply=%region_5.6 | all-reduce | flops 1280 | bytes 10240 | tf_op jit(solution)/shard_map/psum | solution.py:122
  350.8 0.2 add_convert_fusion
  351.0 0.8 copy.19
  (103 shorter events, 1.2 us)
Async XLA Ops:
  0.0 1.0 copy-start
  0.0 32.8 %copy-start.4 = (bf16[512,128]{1,0:T(8,128)(2,1)S(1)}, bf16[512,128]{1,0:T(8,128)(2,1)}, u32[]{:S(2)}) copy-start(bf16[512,128]{1,0:T(8,128)(2,1)} %param.24) | copy-start | bytes 393220
  32.8 19.7 %copy-start.7 = (s32[22528]{0:T(1024)S(1)}, s32[22528]{0:T(1024)}, u32[]{:S(2)}) copy-start(s32[22528]{0:T(1024)} %param.23) | copy-start | bytes 270340
  32.8 19.7 %copy-start.8 = (s32[22528]{0:T(1024)S(1)}, s32[22528]{0:T(1024)}, u32[]{:S(2)}) copy-start(s32[22528]{0:T(1024)} %param.22) | copy-start | bytes 270340
  32.8 19.9 %copy-start.3 = (bf16[640,128]{1,0:T(8,128)(2,1)S(1)}, bf16[640,128]{1,0:T(8,128)(2,1)}, u32[]{:S(2)}) copy-start(bf16[640,128]{1,0:T(8,128)(2,1)} %param.20) | copy-start | bytes 491524
  32.8 43.6 %copy-start.5 = (bf16[512,128]{1,0:T(8,128)(2,1)S(1)}, bf16[512,128]{1,0:T(8,128)(2,1)}, u32[]{:S(2)}) copy-start(bf16[512,128]{1,0:T(8,128)(2,1)} %param.25) | copy-start | bytes 393220
  46.3 3.0 copy-start.2
  50.5 26.3 %collective-permute-start = (bf16[4,640,128]{2,1,0:T(8,128)(2,1)}, bf16[4,640,128]{2,1,0:T(8,128)(2,1)S(1)}, u32[]{:S(2)}, u32[]{:S(2)}) collective-permute-start(bf16[4,640,128]{2,1,0:T(8,128)(2,1)} %bitcast), channel_id=1, source_target_pairs={{0,4},{4,8},{8,12},{12,16},{16,20},{20,24},{24,28},{28,32},{32,36}... | collective-permute-start | bytes 1966088 | tf_op jit(solution)/shard_map/ppermute | solution.py:16
  51.9 24.8 %collective-permute-start.1 = (bf16[4,640,128]{2,1,0:T(8,128)(2,1)}, bf16[4,640,128]{2,1,0:T(8,128)(2,1)S(1)}, u32[]{:S(2)}, u32[]{:S(2)}) collective-permute-start(bf16[4,640,128]{2,1,0:T(8,128)(2,1)} %bitcast.2), channel_id=1, source_target_pairs={{4,0},{8,4},{12,8},{16,12},{20,16},{24,20},{28,24},{32,28},{36,32}... | collective-permute-start | bytes 1966088 | tf_op jit(solution)/shard_map/ppermute | solution.py:19
  81.1 6.2 %copy-start.11 = (bf16[4,128]{1,0:T(4,128)(2,1)S(1)}, bf16[4,128]{1,0:T(4,128)(2,1)}, u32[]{:S(2)}) copy-start(bf16[4,128]{1,0:T(4,128)(2,1)} %param.26) | copy-start | bytes 3076
  81.1 6.2 %copy-start.12 = (f32[128]{0:T(128)S(1)}, f32[128]{0:T(128)}, u32[]{:S(2)}) copy-start(f32[128]{0:T(128)} %param.27) | copy-start | bytes 1540
  87.3 231.8 %copy-start.6 = (bf16[128,512]{1,0:T(8,128)(2,1)S(1)}, bf16[128,512]{1,0:T(8,128)(2,1)}, u32[]{:S(2)}) copy-start(bf16[128,512]{1,0:T(8,128)(2,1)} %param.28) | copy-start | bytes 393220
  87.3 263.5 %copy-start.9 = (f32[128]{0:T(128)S(1)}, f32[128]{0:T(128)}, u32[]{:S(2)}) copy-start(f32[128]{0:T(128)} %param.31) | copy-start | bytes 1540
  87.3 263.5 %copy-start.10 = (f32[128]{0:T(128)S(1)}, f32[128]{0:T(128)}, u32[]{:S(2)}) copy-start(f32[128]{0:T(128)} %param.30) | copy-start | bytes 1540
  319.1 32.7 %copy-start.1 = (bf16[474,512]{1,0:T(8,128)(2,1)S(1)}, bf16[474,512]{1,0:T(8,128)(2,1)}, u32[]{:S(2)}) copy-start(bf16[474,512]{1,0:T(8,128)(2,1)} %param.18) | copy-start | bytes 1456132
  320.9 22.3 %all-to-all-start = ((f32[4,640,128]{1,2,0:T(8,128)}), f32[4,640,128]{1,2,0:T(8,128)S(1)}, u32[]{:S(2)}, u32[]{:S(2)}) async-start(f32[4,640,128]{1,2,0:T(8,128)} %bitcast.7), calls=%async_computation | async-start | bytes 2621440 | tf_op jit(solution)/shard_map/all_to_all | solution.py:31
where the time goes:
time: 353 us; the launch traced here: 352 us
  local copies, waits for them, and re-layouts  193 us (55%)
  matrix products  84.4 us (24%)
  blocking collectives  31 us (9%)
  other arithmetic  19.2 us (5%)
  waiting for transfers between devices  17.8 us (5%)
  starting transfers between devices  5.56 us (2%)
    gather x11, local copies, waits for them, and re-layouts, accumulate(): jnp.take(sent_terms, send_ids, axis=0)  125 us
    gather x11, local copies, waits for them, and re-layouts, accumulate(): jnp.take(recv_terms, recv_ids, axis=0)  60.1 us
    dot_general x11, matrix products, accumulate(): lax.dot_general(one_hot, hidden, (((0,), (0,)), ((), ())), preferred_elem...  37.1 us
    dot_general x1, matrix products, embedded(): jnp.dot(grid_rows, embed_weight, preferred_element_type=jnp.float32)  31.8 us
    all_gather x1, blocking collectives, on_device(): full_mesh = lax.all_gather(mesh_latent, 'ch', axis=1, tiled=True)  23.7 us
    all_to_all x1, waiting for transfers between devices, sent_and_summed(): lax.all_to_all(split_up(value, dim, devices), axis, 0, 0, tiled=True)  17.8 us
    dot_general x1, matrix products, on_device(): jnp.dot(latent, sender_weight, preferred_element_type=jnp.float32)  13.5 us
    reduce_sum x11, other arithmetic, accumulate(): tallies = tallies + jnp.sum(one_hot, axis=0, dtype=jnp.float32)  7.46 us
  transfers between devices with their start and end apart: 3, of which 1 were waited for; matrix products, arithmetic and copies ran while one was open for 0% of the time, Pallas kernels for 0%

commit v1 on v0

v1 whole, which is shorter than its diff:
```python
import functools

import jax
import jax.numpy as jnp
from jax import lax
from jax.experimental import pallas as pl
from jax.experimental.pallas import tpu as pltpu
from jax.sharding import PartitionSpec as P

LAT = 640
HALO = 4
CHUNK = 512
RUN_CHUNKS = 4
SLOTS = 4
WINDOW = 7
PITCH = CHUNK + 8
UNROLL = 32

f32 = jnp.float32
bf16 = jnp.bfloat16


def silu(value):
    half = 0.5 * value
    return half + half * jnp.tanh(half)


def dot(left, right):
    return jnp.dot(left, right, preferred_element_type=f32)


def wide_row(ref, index):
    return ref[pl.ds(pl.multiple_of(index * 4, 4), 4), :]


def chunk_of(tile):
    return jnp.concatenate([tile[j * PITCH : j * PITCH + CHUNK, :] for j in range(4)], axis=1)


def list_chunks(chunks, first_chunk, low_ref, high_ref, own_columns, outer, chunk_list):
    def step(i, count):
        low = low_ref[first_chunk + i]
        high = high_ref[first_chunk + i]
        halo = (low < HALO) | (high >= HALO + own_columns)
        mine = halo if outer else jnp.logical_not(halo)

        @pl.when(mine)
        def _():
            chunk_list[count] = i

        return count + jnp.where(mine, 1, 0)

    return lax.fori_loop(0, chunks, step, 0)


def list_columns(count, first_chunk, low_ref, high_ref, chunk_list, column_list, offset_list):
    slot0 = lax.shift_right_logical(first_chunk, 2)
    total = jnp.int32(0)
    seg_first = jnp.int32(1000)
    seg_last = jnp.int32(-1)
    seg_start = jnp.int32(0)
    for slot in range(SLOTS):

        def step(t, carry):
            low, high = carry
            g = first_chunk + chunk_list[t]
            here = lax.shift_right_logical(g, 2) == slot0 + slot
            return (
                jnp.where(here, jnp.minimum(low, low_ref[g]), low),
                jnp.where(here, jnp.maximum(high, high_ref[g]), high),
            )

        low, high = lax.fori_loop(0, count, step, (jnp.int32(1000), jnp.int32(-1)))
        has = high >= 0
        joins = has & (low >= seg_first) & (low <= seg_last + 1)
        begin = jnp.where(joins, seg_last + 1, low)
        fresh = jnp.where(has, jnp.maximum(high - begin + 1, 0), 0)
        base = total

        def put(j, carry):
            column_list[base + j] = begin + j
            return carry

        lax.fori_loop(0, fresh, put, 0)
        opens = has & jnp.logical_not(joins)
        seg_start = jnp.where(opens, total, seg_start)
        seg_first = jnp.where(opens, low, seg_first)
        seg_last = jnp.where(opens, high, jnp.maximum(seg_last, high))
        total = total + fresh
        offset_list[slot] = (seg_start - seg_first) * LAT
    return total


def embed_kernel(outer, chunks, own_columns, channels, *refs):
    if outer:
        (place, points, low_ref, high_ref, grid, low_own, low_swap, high_own, high_swap,
         weight, bias, _, out) = refs[:13]
        rest = refs[13:]
    else:
        place, points, low_ref, high_ref, grid, weight, bias, out = refs[:8]
        rest = refs[8:]
    table, columns, tile, result, chunk_list, column_list, offset_list, in_sems, out_sems = rest
    first_chunk = place[0] * chunks
    core = place[1]
    count = list_chunks(chunks, first_chunk, low_ref, high_ref, own_columns, outer, chunk_list)
    total = list_columns(
        count, first_chunk, low_ref, high_ref, chunk_list, column_list, offset_list
    )

    def fetch(source, column, slot):
        start = pl.multiple_of(column * LAT, 128)
        pltpu.make_async_copy(
            source.at[:, pl.ds(start, LAT)], columns.at[slot], in_sems.at[slot]
        ).start()

    def start_column(i):
        column = column_list[i]
        slot = lax.rem(i, 2)
        if not outer:
            fetch(grid, column - HALO, slot)
            return
        inside = (column >= HALO) & (column < HALO + own_columns)

        @pl.when(inside)
        def _():
            fetch(grid, column - HALO, slot)

        for is_side, shift, direct, swapped in (
            (column < HALO, 0, low_own, low_swap),
            (column >= HALO + own_columns, HALO + own_columns, high_own, high_swap),
        ):
            place_in = column - shift
            half = lax.shift_right_arithmetic(place_in, 1)
            within = lax.bitwise_and(place_in, 1)

            @pl.when(is_side & (half == core))
            def _():
                fetch(direct, within, slot)

            @pl.when(is_side & (half != core))
            def _():
                fetch(swapped, within, slot)

    @pl.when(total > 0)
    def _():
        start_column(0)

    def turn(i, carry):
        slot = lax.rem(i, 2)

        @pl.when(i + 1 < total)
        def _():
            start_column(i + 1)

        pltpu.make_async_copy(
            grid.at[:, pl.ds(0, LAT)], columns.at[slot], in_sems.at[slot]
        ).wait()
        source = columns.at[slot]
        for l in range(LAT // 128):
            lanes = pl.ds(l * 128, 128)
            for j in range(4):
                top = min(channels, (j + 1) * 128)
                block = source[j * 128 : top, lanes]
                if top < (j + 1) * 128:
                    block = jnp.pad(block, ((0, (j + 1) * 128 - top), (0, 0)))
                row = pl.multiple_of((i * LAT + l * 128) * 4, 8)
                table[pl.ds(row + j, 128, stride=4), :] = block.T.astype(f32)
        return carry

    lax.fori_loop(0, total, turn, 0)

    def work(t, carry):
        i = chunk_list[t]
        g = first_chunk + i
        offset = offset_list[
            lax.shift_right_logical(g, 2) - lax.shift_right_logical(first_chunk, 2)
        ]
        edge0 = g * CHUNK

        def gather(b, inner):
            for u in range(UNROLL):
                e = b * UNROLL + u
                tile[pl.ds(e, 4, stride=PITCH), :] = wide_row(table, points[edge0 + e] + offset)
            return inner

        lax.fori_loop(0, CHUNK // UNROLL, gather, 0)
        slot = lax.rem(t, 2)
        latent = silu(dot(chunk_of(tile).astype(bf16), weight[...]) + bias[...]).astype(bf16)

        @pl.when(t >= 2)
        def _():
            pltpu.make_async_copy(
                result.at[slot], out.at[pl.ds(0, CHUNK)], out_sems.at[slot]
            ).wait()

        result[slot] = latent
        pltpu.make_async_copy(
            result.at[slot],
            out.at[pl.ds(pl.multiple_of(i * CHUNK, CHUNK), CHUNK)],
            out_sems.at[slot],
        ).start()
        return carry

    lax.fori_loop(0, count, work, 0)
    for back in (2, 1):

        @pl.when(count >= back)
        def _():
            slot = lax.rem(count - back, 2)
            pltpu.make_async_copy(
                result.at[slot], out.at[pl.ds(0, CHUNK)], out_sems.at[slot]
            ).wait()


def edge_kernel(chunks, nodes, place, receivers, latent, ids, features, w0, w1, w2, w3,
                m0, m1, m2, m3, message_bias, keep, send,
                rows, tile, arrived, send_weight, recv_weight, message_weight, mesh, feature_weight,
                totals, tally, sems):
    k = place[0]
    first_chunk = k * chunks

    def start(t):
        slot = lax.rem(t, 2)
        pltpu.make_async_copy(
            latent.at[pl.ds(pl.multiple_of(t * CHUNK, CHUNK), CHUNK)], arrived.at[slot], sems.at[slot]
        ).start()

    start(0)
    biases = []
    for j, (w, m) in enumerate(((w0, m0), (w1, m1), (w2, m2), (w3, m3))):
        lanes = pl.ds(j * 128, 128)
        send_weight[:, lanes] = w[0:512, :]
        recv_weight[:, lanes] = w[512:1024, :]
        for q in range(4):
            message_weight[j * 128 : (j + 1) * 128, q * 128 : (q + 1) * 128] = w[
                1024 + q * 128 : 1024 + (q + 1) * 128, :
            ]
        extra = w[1536:1552, :].astype(f32)
        feature_weight[0:4, lanes] = extra[0:4, :]
        biases.append(extra[4:5, :] + extra[5:6, :] + extra[6:7, :])
        at = pl.multiple_of(jnp.bitwise_xor(k, j) * 128, 128)
        mesh[:, pl.ds(at, 128)] = m[...]
    bias = jnp.concatenate(biases, axis=1)
    terms = dot(mesh[...], recv_weight[...]) + bias
    for j in range(4):
        rows[pl.ds(j, nodes, stride=4), :] = terms[:, j * 128 : (j + 1) * 128]
    totals[...] = jnp.zeros_like(totals)
    tally[...] = jnp.zeros_like(tally)
    features_by = feature_weight[...].astype(bf16)

    def work(t, carry):
        slot = lax.rem(t, 2)
        g = first_chunk + t
        edge0 = g * CHUNK

        @pl.when(t + 1 < chunks)
        def _():
            start(t + 1)

        def gather(b, inner):
            for u in range(UNROLL):
                e = b * UNROLL + u
                tile[pl.ds(e, 4, stride=PITCH), :] = wide_row(rows, receivers[edge0 + e])
            return inner

        lax.fori_loop(0, CHUNK // UNROLL, gather, 0)
        pltpu.make_async_copy(
            latent.at[pl.ds(0, CHUNK)], arrived.at[slot], sems.at[slot]
        ).wait()
        before = (
            dot(arrived[slot], send_weight[...])
            + chunk_of(tile)
            + lax.dot_general(
                features[g], features_by, (((0,), (0,)), ((), ())), preferred_element_type=f32
            )
        )
        hidden = silu(before).astype(bf16)
        hot = jnp.where(
            lax.broadcasted_iota(jnp.int32, (nodes, CHUNK), 0) == ids[pl.ds(g, 1), :], 1.0, 0.0
        )
        totals[...] += dot(hot.astype(bf16), hidden)
        tally[...] += (hot[:, 0:128] + hot[:, 128:256]) + (hot[:, 256:384] + hot[:, 384:512])
        return carry

    lax.fori_loop(0, chunks, work, 0)
    counts = jnp.sum(tally[...], axis=1, keepdims=True)
    whole = totals[...]
    upper = whole.astype(bf16)
    lower = (whole - upper.astype(f32)).astype(bf16)
    totals[...] = (
        dot(upper, message_weight[...])
        + dot(lower, message_weight[...])
        + counts * message_bias[...]
    )
    for r in range(2):
        mine = pl.multiple_of(jnp.bitwise_xor(k, 2 * r) * 128, 128)
        theirs = pl.multiple_of(jnp.bitwise_xor(k, 2 * r + 1) * 128, 128)
        keep[r] = totals[:, pl.ds(mine, 128)]
        send[r] = totals[:, pl.ds(theirs, 128)]


VMEM = pl.BlockSpec(memory_space=pltpu.VMEM)
SMEM = pl.BlockSpec(memory_space=pltpu.SMEM)
ANY = pl.BlockSpec(memory_space=pl.ANY)


def embed_call(outer, chunks, own_columns, channels, operands):
    width = 512
    count = len(operands)
    specs = [SMEM] * 4 + [ANY] * (5 if outer else 1) + [VMEM] * 2
    if outer:
        specs = specs + [ANY]
    slots = SLOTS * WINDOW
    return pl.pallas_call(
        functools.partial(embed_kernel, outer, chunks, own_columns, channels),
        out_shape=jax.ShapeDtypeStruct((chunks * CHUNK, width), bf16),
        in_specs=specs,
        out_specs=ANY,
        input_output_aliases={count - 1: 0} if outer else {},
        scratch_shapes=[
            pltpu.VMEM((slots * LAT * 4, 128), f32),
            pltpu.VMEM((2, channels, LAT), bf16),
            pltpu.VMEM((4 * PITCH, 128), f32),
            pltpu.VMEM((2, CHUNK, width), bf16),
            pltpu.SMEM((16,), jnp.int32),
            pltpu.SMEM((32,), jnp.int32),
            pltpu.SMEM((8,), jnp.int32),
            pltpu.SemaphoreType.DMA((2,)),
            pltpu.SemaphoreType.DMA((2,)),
        ],
        compiler_params=pltpu.CompilerParams(vmem_limit_bytes=60 * 2**20),
        name="embed_outer" if outer else "embed_inner",
    )(*operands)


def edge_call(chunks, nodes, operands):
    width = 512
    part = jax.ShapeDtypeStruct((2, nodes, 128), f32)
    return pl.pallas_call(
        functools.partial(edge_kernel, chunks, nodes),
        out_shape=(part, part),
        in_specs=[SMEM] * 2 + [ANY] + [VMEM] * 11,
        out_specs=(VMEM, VMEM),
        scratch_shapes=[
            pltpu.VMEM((nodes * 4, 128), f32),
            pltpu.VMEM((4 * PITCH, 128), f32),
            pltpu.VMEM((2, CHUNK, width), bf16),
            pltpu.VMEM((width, width), bf16),
            pltpu.VMEM((width, width), bf16),
            pltpu.VMEM((width, width), bf16),
            pltpu.VMEM((nodes, width), bf16),
            pltpu.VMEM((4, width), f32),
            pltpu.VMEM((nodes, width), f32),
            pltpu.VMEM((nodes, 128), f32),
            pltpu.SemaphoreType.DMA((2,)),
        ],
        compiler_params=pltpu.CompilerParams(vmem_limit_bytes=56 * 2**20),
        name="edges",
    )(*operands)


def on_device(
    grid_inputs,
    embed_weight,
    embed_bias,
    mesh_latent,
    edge_features,
    senders,
    receivers,
    sender_weight,
    receiver_weight,
    feature_weight,
    hidden_bias,
    message_weight,
    message_bias,
    norm_gain,
    norm_shift,
):
    lon_count = lax.axis_size("lon")
    ch_count = lax.axis_size("ch")
    lon_place = lax.axis_index("lon")
    ch_place = lax.axis_index("ch")
    core = lax.bitwise_and(ch_place, 1)
    place = jnp.stack([ch_place, core]).astype(jnp.int32)
    points_own, channels = grid_inputs.shape
    own_columns = points_own // LAT
    mesh_nodes = mesh_latent.shape[0]
    full_width = message_weight.shape[1]
    edge_count = senders.shape[0]
    all_chunks = edge_count // CHUNK
    chunks = all_chunks // ch_count

    swap = [(i, i ^ 1) for i in range(ch_count)]
    across = [(i, i ^ 2) for i in range(ch_count)]
    facing = [
        (lon * ch_count + ch, (lon ^ 4) * ch_count + (ch ^ 2))
        for lon in range(lon_count)
        for ch in range(ch_count)
    ]
    forward = [(i, (i + 1) % lon_count) for i in range(lon_count)]
    backward = [(target, source) for source, target in forward]

    flat = grid_inputs.T
    half_points = HALO * LAT // 2
    low_half = lax.dynamic_slice_in_dim(
        flat, points_own - 2 * half_points + core * half_points, half_points, 1
    )
    high_half = lax.dynamic_slice_in_dim(flat, core * half_points, half_points, 1)
    low_own = lax.ppermute(low_half, "lon", forward)
    high_own = lax.ppermute(high_half, "lon", backward)
    low_swap = lax.ppermute(low_own, "ch", swap)
    high_swap = lax.ppermute(high_own, "ch", swap)

    part0 = lax.reduce_precision(hidden_bias, 8, 7)
    part1 = lax.reduce_precision(hidden_bias - part0, 8, 7)
    part2 = lax.reduce_precision(hidden_bias - part0 - part1, 8, 7)
    share = message_weight.shape[0]
    bundle = jnp.concatenate(
        [sender_weight, receiver_weight]
        + [message_weight[:, q * share : (q + 1) * share] for q in range(ch_count)]
        + [feature_weight, jnp.stack([part0, part1, part2]).astype(bf16)]
        + [jnp.zeros((9, share), bf16)],
        axis=0,
    )
    bundle_far = lax.ppermute(bundle, ("lon", "ch"), facing)
    bundle_near = lax.ppermute(bundle, "ch", swap)
    bundle_last = lax.ppermute(bundle_far, "ch", swap)
    mesh_far = lax.ppermute(mesh_latent, "ch", across)
    mesh_near = lax.ppermute(mesh_latent, "ch", swap)
    mesh_last = lax.ppermute(mesh_far, "ch", swap)

    points = jnp.mod(
        senders - lon_place * points_own + HALO * LAT, points_own * lon_count
    )
    by_chunk = points.reshape(all_chunks, CHUNK)
    low_column = jnp.min(by_chunk, axis=1) // LAT
    high_column = jnp.max(by_chunk, axis=1) // LAT
    local_recv = receivers - lon_place * mesh_nodes

    weight = jnp.pad(embed_weight, ((0, full_width - channels), (0, 0)))
    common = [place, points, low_column, high_column, flat]
    latent = embed_call(
        False, chunks, own_columns, channels, common + [weight, embed_bias[None, :]]
    )
    latent = embed_call(
        True, chunks, own_columns, channels,
        common + [low_own, low_swap, high_own, high_swap, weight, embed_bias[None, :], latent],
    )
    feature_blocks = jnp.transpose(
        edge_features.reshape(edge_features.shape[0], all_chunks, CHUNK), (1, 0, 2)
    )
    keep, send = edge_call(
        chunks, mesh_nodes,
        [place, local_recv, latent, local_recv.reshape(all_chunks, CHUNK), feature_blocks,
         bundle, bundle_near, bundle_far, bundle_last,
         mesh_latent, mesh_near, mesh_far, mesh_last, message_bias[None, :]],
    )
    halves = keep + lax.ppermute(send, "ch", swap)
    node_share = halves[0] + lax.ppermute(halves[1], "ch", across)
    first_sum, second = lax.psum(
        (
            jnp.sum(node_share, axis=1, keepdims=True),
            jnp.sum(jnp.square(node_share), axis=1, keepdims=True),
        ),
        "ch",
    )
    centre = first_sum / full_width
    spread = second / full_width - jnp.square(centre)
    normed = (node_share - centre) * lax.rsqrt(spread + 1.0)
    return (mesh_latent.astype(f32) + normed * norm_gain + norm_shift).astype(bf16)


def solution(mesh):
    return jax.shard_map(
        on_device,
        mesh=mesh,
        in_specs=(
            P("lon", None),
            P(),
            P(),
            P("lon", "ch"),
            P(None, "lon"),
            P("lon"),
            P("lon"),
            P(None, "ch"),
            P(None, "ch"),
            P(None, "ch"),
            P("ch"),
            P("ch", None),
            P(),
            P("ch"),
            P("ch"),
        ),
        out_specs=P("lon", "ch"),
        check_vma=False,
    )
```

time: 353 us -> 134 us (0.38)
  local copies, waits for them, and re-layouts: 193 us -> 6.32 us
  matrix products: 84.4 us -> 0 us
  Pallas kernels: 0 us -> 61.7 us
  waiting for transfers between devices: 17.8 us -> 45.6 us
  blocking collectives: 31 us -> 7.34 us
  other arithmetic: 19.2 us -> 4.67 us
    gather x22 -> x0, local copies, waits for them, and re-layouts: 185 us -> none  [the longest x11 125 us: accumulate(): jnp.take(sent_terms, send_ids, axis=0)]
    dot_general x15 -> x0, matrix products: 84.4 us -> none  [the longest x11 37.1 us: accumulate(): lax.dot_general(one_hot, hidden, (((0,), (0,)), ((), ())), preferred_elem...]
    pallas_call x0 -> x3, Pallas kernels: none -> 61.7 us  [the longest x2 35.6 us: embed_call(): pl.pallas_call(functools.partial(embed_kernel, outer, chunks, own_columns...]
    ppermute x2 -> x12, waiting for transfers between devices: 0.01 us -> 45.6 us  [the longest x1 22.8 us: on_device(): low_own = lax.ppermute(low_half, 'lon', forward)]
    all_gather x1 -> x0, blocking collectives: 23.7 us -> none  [on_device(): full_mesh = lax.all_gather(mesh_latent, 'ch', axis=1, tiled=True)]
    all_to_all x1 -> x0, waiting for transfers between devices: 17.8 us -> none  [sent_and_summed(): lax.all_to_all(split_up(value, dim, devices), axis, 0, 0, tiled=True)]
    reduce_sum x12 -> x0, other arithmetic: 7.55 us -> none  [the longest x11 7.46 us: accumulate(): tallies = tallies + jnp.sum(one_hot, axis=0, dtype=jnp.float32)]
    convert_element_type x2 -> x1, other arithmetic: 6.36 us -> 0.91 us  [on_device(): (mesh_latent.astype(f32) + normed * norm_gain + norm_shift).astype(bf16)]
  transfers between devices with their start and end apart: 3 -> 12, of which waited for: 1 -> 5; matrix products, arithmetic and copies ran while one was open for 0% -> 4% of each run, Pallas kernels for 0% -> 27%
where the time goes in v1:
time: 134 us; the launch traced here: 133 us
  Pallas kernels  61.7 us (46%)
  waiting for transfers between devices  45.6 us (34%)
  blocking collectives  7.34 us (5%)
  starting transfers between devices  6.94 us (5%)
  local copies, waits for them, and re-layouts  6.32 us (5%)
  other arithmetic  4.67 us (3%)
    pallas_call x2, Pallas kernels, embed_call(): pl.pallas_call(functools.partial(embed_kernel, outer, chunks, own_columns...  35.6 us
    pallas_call x1, Pallas kernels, edge_call(): pl.pallas_call(functools.partial(edge_kernel, chunks, nodes), out_shape=(...  26.2 us
    ppermute x1, waiting for transfers between devices, on_device(): low_own = lax.ppermute(low_half, 'lon', forward)  22.8 us
    ppermute x1, waiting for transfers between devices, on_device(): node_share = halves[0] + lax.ppermute(halves[1], 'ch', across)  11.2 us
    psum x1, blocking collectives, on_device(): lax.psum((jnp.sum(node_share, axis=1, keepdims=True), jnp.sum(jnp.square(...  7.34 us
    ppermute x1, waiting for transfers between devices, on_device(): mesh_far = lax.ppermute(mesh_latent, 'ch', across)  5.79 us
    ppermute x1, waiting for transfers between devices, on_device(): high_own = lax.ppermute(high_half, 'lon', backward)  3.41 us
    dynamic_slice x1, local copies, waits for them, and re-layouts, on_device(): lax.dynamic_slice_in_dim(flat, core * half_points, half_points, 1)  3.39 us
  transfers between devices with their start and end apart: 12, of which 5 were waited for; matrix products, arithmetic and copies ran while one was open for 4% of the time, Pallas kernels for 27%

profile of v1, /device:TPU:6, one launch (start us, length us, event | category | flops | bytes accessed | tf_op | source)
XLA Modules:
  0.0 132.9 jit_solution(18076644009554967298)
XLA Ops:
  0.0 0.0 copy-start.15
  0.0 0.0 copy-start.8
  0.0 0.0 copy-start.10
  0.0 0.0 copy-start.12
  0.0 0.0 copy-start.5
  0.0 0.0 copy-start.11
  0.1 3.4 %dynamic-slice_bitcast_fusion = (bf16[474,1280]{1,0:T(8,128)(2,1)}, bf16[474,1280]{1,0:T(8,128)(2,1)}) fusion(bf16[28800,474]{0,1:T(8,128)(2,1)} %param.15, s32[]{:T(128)S(6)} %select_n.25, s32[]{:T(128)S(6)} %select_n.24), kind=kLoop, calls=%fused_computation | loop fusion | bytes 4853768 | tf_op jit(solution)/shard_map/dynamic_slice | solution.py:408
  3.4 1.5 %collective-permute-start = (bf16[474,1280]{1,0:T(8,128)(2,1)}, bf16[474,1280]{1,0:T(8,128)(2,1)S(1)}, u32[]{:S(2)}, u32[]{:S(2)}) collective-permute-start(bf16[474,1280]{1,0:T(8,128)(2,1)} %get-tuple-element.18), channel_id=1, source_target_pairs={{0,4},{4,8},{8,12},{12,16},{16,20},{20,24},{24,28},{28,32},{32,36}... | collective-permute-start | bytes 3640328 | tf_op jit(solution)/shard_map/ppermute | solution.py:409
  4.9 0.5 collective-permute-start.2
  5.5 0.0 copy-done.15
  5.5 0.0 copy-done.8
  5.5 0.0 copy-done.9
  5.5 0.0 copy-done.10
  5.5 0.0 copy-done.12
  5.6 0.3 concatenate.4.w0
  5.8 0.0 copy-start
  5.8 3.1 %collective-permute-start.5 = (bf16[1552,128]{1,0:T(8,128)(2,1)S(1)}, bf16[1552,128]{1,0:T(8,128)(2,1)}, u32[]{:S(2)}, u32[]{:S(2)}) collective-permute-start(bf16[1552,128]{1,0:T(8,128)(2,1)S(1)} %concatenate.4.w0), channel_id=1, source_target_pairs={{0,18},{1,19},{2,16},{3,17},{4,22},{5,23},{6,20},{7,21},{8,26},{9,... | collective-permute-start | bytes 1191944 | tf_op jit(solution)/shard_map/ppermute | solution.py:425
  8.9 0.0 collective-permute-start.4
  8.9 0.0 copy-done.5
  8.9 0.6 collective-permute-start.8
  9.6 22.8 %collective-permute-done.refs_5_ = bf16[474,1280]{1,0:T(8,128)(2,1)S(1)} collective-permute-done((bf16[474,1280]{1,0:T(8,128)(2,1)}, bf16[474,1280]{1,0:T(8,128)(2,1)S(1)}, u32[]{:S(2)}, u32[]{:S(2)}) %collective-permute-start) | collective-permute-done | bytes 1213472 | tf_op jit(solution)/shard_map/ppermute | solution.py:409
  32.4 0.0 collective-permute-start.1
  32.4 3.4 %collective-permute-done.2.refs_7_ = bf16[474,1280]{1,0:T(8,128)(2,1)S(1)} collective-permute-done((bf16[474,1280]{1,0:T(8,128)(2,1)}, bf16[474,1280]{1,0:T(8,128)(2,1)S(1)}, u32[]{:S(2)}, u32[]{:S(2)}) %collective-permute-start.2) | collective-permute-done | bytes 1213472 | tf_op jit(solution)/shard_map/ppermute | solution.py:410
  35.8 0.0 collective-permute-start.3
  35.8 0.0 copy-done.11
  35.8 0.1 add_select_fusion.refs_1_
  35.9 0.0 copy-start.1
  35.9 1.0 broadcast_subtract_fusion.receivers
  37.0 0.0 collective-permute-done.5.w2
  37.0 0.5 collective-permute-start.6
  37.5 0.1 fusion.7
  37.6 5.8 %collective-permute-done.8.m2 = bf16[640,128]{1,0:T(8,128)(2,1)S(1)} collective-permute-done((bf16[640,128]{1,0:T(8,128)(2,1)S(1)}, bf16[640,128]{1,0:T(8,128)(2,1)S(1)}, u32[]{:S(2)}, u32[]{:S(2)}) %collective-permute-start.8) | collective-permute-done | bytes 163872 | tf_op jit(solution)/shard_map/ppermute | solution.py:428
  43.4 0.0 collective-permute-start.7
  43.4 0.0 collective-permute-done.1.refs_6_
  43.4 0.5 collective-permute-start.9
  43.9 0.5 and_select_fusion
  44.4 1.9 %pad.4.refs_5_.refs_9_ = bf16[512,512]{1,0:T(8,128)(2,1)} pad(bf16[474,512]{1,0:T(8,128)(2,1)} %param.16, bf16[]{:T(256)} %constant.57.clone.1), padding=0_38x0_0 | pad | bytes 1009666 | tf_op jit(solution)/shard_map/jit(_pad)/pad | solution.py:440
  46.3 0.7 reshape.12.ids
  47.0 0.6 pad_add_fusion.refs_0_.place
  47.5 0.0 copy-done.1
  47.5 21.9 %embed_inner.1.refs_11_ = bf16[5632,512]{1,0:T(8,128)(2,1)} custom-call(s32[2]{0:T(128)} %pad_add_fusion.refs_0_.place, s32[22528]{0:T(1024)} %copy-done.1, s32[44]{0:T(128)} %get-tuple-element.27.refs_2_, s32[44]{0:T(128)} %get-tuple-element.26.refs_3_, bf16[474,28800]{1,0:T(8,128)(2,1)} %bitcast.30, bf16[512,512]{1,0:T(8,128)(2,1)} %pad.4.refs_5_.refs_9_, ...), custom_call_target="tpu_custom_call" | custom-call | tf_op jit(solution)/shard_map/embed_inner/pallas_call | solution.py:314
  69.5 0.0 copy-done
  69.5 0.0 copy-done.2
  69.5 0.0 copy-done.3
  69.5 0.0 copy-done.4
  69.5 0.0 copy-done.7
  69.5 0.0 collective-permute-done.3.refs_8_
  69.5 13.7 %embed_outer.1.latent = bf16[5632,512]{1,0:T(8,128)(2,1)} custom-call(s32[2]{0:T(128)} %pad_add_fusion.refs_0_.place, s32[22528]{0:T(1024)} %copy-done.1, s32[44]{0:T(128)} %get-tuple-element.27.refs_2_, s32[44]{0:T(128)} %get-tuple-element.26.refs_3_, bf16[474,28800]{1,0:T(8,128)(2,1)} %bitcast.31, ...), custom_call_target="tpu_custom_call", output_to_operand_aliasing={{}: (11, {})} | custom-call | tf_op jit(solution)/shard_map/embed_outer/pallas_call | solution.py:314
  83.2 0.0 collective-permute-done.7.m1
  83.2 0.0 collective-permute-done.9.m3
  83.2 0.0 collective-permute-done.4.w1
  83.2 0.0 collective-permute-done.6.w3
  83.2 26.2 %edges.1 = (f32[2,640,128]{2,1,0:T(8,128)}, f32[2,640,128]{2,1,0:T(8,128)}) custom-call(s32[2]{0:T(128)} %pad_add_fusion.refs_0_.place, s32[22528]{0:T(1024)} %copy-done.4, bf16[5632,512]{1,0:T(8,128)(2,1)} %embed_outer.1.latent, s32[44,512]{1,0:T(8,128)} %reshape.12.ids, bf16[44,4,512]{2,1,0:T(4,128)(2,1)} %bitcast.32, bf16[1552,128]{1,0:T(8,128)(2,1)} %copy-done, ...), custom_call_target="tpu_custom_call" | custom-call | tf_op jit(solution)/shard_map/edges/pallas_call | solution.py:339
  109.4 0.1 collective-permute-start.10
  109.5 2.3 %collective-permute-done.10 = f32[2,640,128]{2,1,0:T(8,128)S(1)} collective-permute-done((f32[2,640,128]{2,1,0:T(8,128)}, f32[2,640,128]{2,1,0:T(8,128)S(1)}, u32[]{:S(2)}, u32[]{:S(2)}) %collective-permute-start.10) | collective-permute-done | bytes 655392 | tf_op jit(solution)/shard_map/ppermute | solution.py:458
  111.8 1.2 add.56
  113.0 0.1 collective-permute-start.11
  113.1 11.2 %collective-permute-done.11 = f32[640,128]{1,0:T(8,128)S(1)} collective-permute-done((f32[640,128]{1,0:T(8,128)S(1)}, f32[640,128]{1,0:T(8,128)S(1)}, u32[]{:S(2)}, u32[]{:S(2)}) %collective-permute-start.11) | collective-permute-done | bytes 327712 | tf_op jit(solution)/shard_map/ppermute | solution.py:459
  124.4 0.2 fusion.6
  124.6 7.3 %all-reduce.1 = (f32[640,1]{0,1:T(1,128)S(1)}, f32[640,1]{0,1:T(1,128)S(1)}) all-reduce(f32[640,1]{0,1:T(1,128)S(1)} %broadcast_in_dim.21, f32[640,1]{0,1:T(1,128)S(1)} %broadcast_in_dim.22), channel_id=1, replica_groups=mesh['lon'=32,'ch'=4] {'ch'}, use_global_device_ids=true, to_apply=%region_3.4 | all-reduce | flops 1280 | bytes 10240 | tf_op jit(solution)/shard_map/psum | solution.py:460
  132.0 0.0 copy-done.6
  132.0 0.0 copy-done.13
  132.0 0.0 copy-done.14
  132.0 0.9 add_convert_fusion
  (16 shorter events, 0.1 us)
Async XLA Ops:
  0.0 5.5 %copy-start.15 = (f32[128]{0:T(128)S(1)}, f32[128]{0:T(128)}, u32[]{:S(2)}) copy-start(f32[128]{0:T(128)} %param.25) | copy-start | bytes 1540
  0.0 5.5 %copy-start.8 = (bf16[128,512]{1,0:T(8,128)(2,1)S(1)}, bf16[128,512]{1,0:T(8,128)(2,1)}, u32[]{:S(2)}) copy-start(bf16[128,512]{1,0:T(8,128)(2,1)} %param.26) | copy-start | bytes 393220
  0.0 5.5 %copy-start.9 = (bf16[512,128]{1,0:T(8,128)(2,1)S(1)}, bf16[512,128]{1,0:T(8,128)(2,1)}, u32[]{:S(2)}) copy-start(bf16[512,128]{1,0:T(8,128)(2,1)} %param.22) | copy-start | bytes 393220
  0.0 5.5 %copy-start.10 = (bf16[512,128]{1,0:T(8,128)(2,1)S(1)}, bf16[512,128]{1,0:T(8,128)(2,1)}, u32[]{:S(2)}) copy-start(bf16[512,128]{1,0:T(8,128)(2,1)} %param.23) | copy-start | bytes 393220
  0.0 5.5 %copy-start.12 = (bf16[4,128]{1,0:T(4,128)(2,1)S(1)}, bf16[4,128]{1,0:T(4,128)(2,1)}, u32[]{:S(2)}) copy-start(bf16[4,128]{1,0:T(4,128)(2,1)} %param.24) | copy-start | bytes 3076
  0.0 8.9 %copy-start.5 = (bf16[640,128]{1,0:T(8,128)(2,1)S(1)}, bf16[640,128]{1,0:T(8,128)(2,1)}, u32[]{:S(2)}) copy-start(bf16[640,128]{1,0:T(8,128)(2,1)} %m0.1) | copy-start | bytes 491524
  0.0 35.8 %copy-start.11 = (s32[22528]{0:T(1024)S(1)}, s32[22528]{0:T(1024)}, u32[]{:S(2)}) copy-start(s32[22528]{0:T(1024)} %param.20) | copy-start | bytes 270340
  3.4 29.0 %collective-permute-start = (bf16[474,1280]{1,0:T(8,128)(2,1)}, bf16[474,1280]{1,0:T(8,128)(2,1)S(1)}, u32[]{:S(2)}, u32[]{:S(2)}) collective-permute-start(bf16[474,1280]{1,0:T(8,128)(2,1)} %get-tuple-element.18), channel_id=1, source_target_pairs={{0,4},{4,8},{8,12},{12,16},{16,20},{20,24},{24,28},{28,32},{32,36}... | collective-permute-start | bytes 3640328 | tf_op jit(solution)/shard_map/ppermute | solution.py:409
  4.9 30.9 %collective-permute-start.2 = (bf16[474,1280]{1,0:T(8,128)(2,1)}, bf16[474,1280]{1,0:T(8,128)(2,1)S(1)}, u32[]{:S(2)}, u32[]{:S(2)}) collective-permute-start(bf16[474,1280]{1,0:T(8,128)(2,1)} %get-tuple-element.17), channel_id=1, source_target_pairs={{4,0},{8,4},{12,8},{16,12},{20,16},{24,20},{28,24},{32,28},{36,32}... | collective-permute-start | bytes 3640328 | tf_op jit(solution)/shard_map/ppermute | solution.py:410
  5.8 63.6 %copy-start = (bf16[1552,128]{1,0:T(8,128)(2,1)}, bf16[1552,128]{1,0:T(8,128)(2,1)S(1)}, u32[]{:S(2)}) copy-start(bf16[1552,128]{1,0:T(8,128)(2,1)S(1)} %concatenate.4.w0) | copy-start | bytes 1191940
  5.8 31.1 %collective-permute-start.5 = (bf16[1552,128]{1,0:T(8,128)(2,1)S(1)}, bf16[1552,128]{1,0:T(8,128)(2,1)}, u32[]{:S(2)}, u32[]{:S(2)}) collective-permute-start(bf16[1552,128]{1,0:T(8,128)(2,1)S(1)} %concatenate.4.w0), channel_id=1, source_target_pairs={{0,18},{1,19},{2,16},{3,17},{4,22},{5,23},{6,20},{7,21},{8,26},{9,... | collective-permute-start | bytes 1191944 | tf_op jit(solution)/shard_map/ppermute | solution.py:425
  8.9 74.3 %collective-permute-start.4 = (bf16[1552,128]{1,0:T(8,128)(2,1)S(1)}, bf16[1552,128]{1,0:T(8,128)(2,1)}, u32[]{:S(2)}, u32[]{:S(2)}) collective-permute-start(bf16[1552,128]{1,0:T(8,128)(2,1)S(1)} %concatenate.4.w0), channel_id=1, source_target_pairs={{0,1},{1,0},{2,3},{3,2},{4,5},{5,4},{6,7},{7,6},{8,9},{9,8},{10,11... | collective-permute-start | bytes 1191944 | tf_op jit(solution)/shard_map/ppermute | solution.py:426
  8.9 34.4 %collective-permute-start.8 = (bf16[640,128]{1,0:T(8,128)(2,1)S(1)}, bf16[640,128]{1,0:T(8,128)(2,1)S(1)}, u32[]{:S(2)}, u32[]{:S(2)}) collective-permute-start(bf16[640,128]{1,0:T(8,128)(2,1)S(1)} %copy-done.5), channel_id=1, source_target_pairs={{0,2},{1,3},{2,0},{3,1},{4,6},{5,7},{6,4},{7,5},{8,10},{9,11},{10,... | collective-permute-start | bytes 491528 | tf_op jit(solution)/shard_map/ppermute | solution.py:428
  32.4 37.1 %copy-start.2 = (bf16[474,1280]{1,0:T(8,128)(2,1)}, bf16[474,1280]{1,0:T(8,128)(2,1)S(1)}, u32[]{:S(2)}) copy-start(bf16[474,1280]{1,0:T(8,128)(2,1)S(1)} %collective-permute-done.refs_5_) | copy-start | bytes 3640324
  32.4 11.0 %collective-permute-start.1 = (bf16[474,1280]{1,0:T(8,128)(2,1)S(1)}, bf16[474,1280]{1,0:T(8,128)(2,1)}, u32[]{:S(2)}, u32[]{:S(2)}) collective-permute-start(bf16[474,1280]{1,0:T(8,128)(2,1)S(1)} %collective-permute-done.refs_5_), channel_id=1, source_target_pairs={{0,1},{1,0},{2,3},{3,2},{4,5},{5,4},{6,7},{7,6},{8,9},{9,8},{10,11... | collective-permute-start | bytes 3640328 | tf_op jit(solution)/shard_map/ppermute | solution.py:411
  35.8 33.7 %copy-start.3 = (bf16[474,1280]{1,0:T(8,128)(2,1)}, bf16[474,1280]{1,0:T(8,128)(2,1)S(1)}, u32[]{:S(2)}) copy-start(bf16[474,1280]{1,0:T(8,128)(2,1)S(1)} %collective-permute-done.2.refs_7_) | copy-start | bytes 3640324
  35.8 33.7 %collective-permute-start.3 = (bf16[474,1280]{1,0:T(8,128)(2,1)S(1)}, bf16[474,1280]{1,0:T(8,128)(2,1)}, u32[]{:S(2)}, u32[]{:S(2)}) collective-permute-start(bf16[474,1280]{1,0:T(8,128)(2,1)S(1)} %collective-permute-done.2.refs_7_), channel_id=1, source_target_pairs={{0,1},{1,0},{2,3},{3,2},{4,5},{5,4},{6,7},{7,6},{8,9},{9,8},{10,11... | collective-permute-start | bytes 3640328 | tf_op jit(solution)/shard_map/ppermute | solution.py:412
  35.9 11.6 %copy-start.1 = (s32[22528]{0:T(1024)}, s32[22528]{0:T(1024)S(1)}, u32[]{:S(2)}) copy-start(s32[22528]{0:T(1024)S(1)} %add_select_fusion.refs_1_) | copy-start | bytes 270340
  36.9 32.6 %copy-start.4 = (s32[22528]{0:T(1024)}, s32[22528]{0:T(1024)S(1)}, u32[]{:S(2)}) copy-start(s32[22528]{0:T(1024)S(1)} %broadcast_subtract_fusion.receivers) | copy-start | bytes 270340
  37.0 46.2 %collective-permute-start.6 = (bf16[1552,128]{1,0:T(8,128)(2,1)}, bf16[1552,128]{1,0:T(8,128)(2,1)}, u32[]{:S(2)}, u32[]{:S(2)}) collective-permute-start(bf16[1552,128]{1,0:T(8,128)(2,1)} %collective-permute-done.5.w2), channel_id=1, source_target_pairs={{0,1},{1,0},{2,3},{3,2},{4,5},{5,4},{6,7},{7,6},{8,9},{9,8},{10,11... | collective-permute-start | bytes 1191944 | tf_op jit(solution)/shard_map/ppermute | solution.py:427
  43.4 26.1 %copy-start.7 = (bf16[640,128]{1,0:T(8,128)(2,1)}, bf16[640,128]{1,0:T(8,128)(2,1)S(1)}, u32[]{:S(2)}) copy-start(bf16[640,128]{1,0:T(8,128)(2,1)S(1)} %collective-permute-done.8.m2) | copy-start | bytes 491524
  43.4 39.8 %collective-permute-start.7 = (bf16[640,128]{1,0:T(8,128)(2,1)S(1)}, bf16[640,128]{1,0:T(8,128)(2,1)}, u32[]{:S(2)}, u32[]{:S(2)}) collective-permute-start(bf16[640,128]{1,0:T(8,128)(2,1)S(1)} %copy-done.5), channel_id=1, source_target_pairs={{0,1},{1,0},{2,3},{3,2},{4,5},{5,4},{6,7},{7,6},{8,9},{9,8},{10,11... | collective-permute-start | bytes 491528 | tf_op jit(solution)/shard_map/ppermute | solution.py:429
  43.4 39.8 %collective-permute-start.9 = (bf16[640,128]{1,0:T(8,128)(2,1)S(1)}, bf16[640,128]{1,0:T(8,128)(2,1)}, u32[]{:S(2)}, u32[]{:S(2)}) collective-permute-start(bf16[640,128]{1,0:T(8,128)(2,1)S(1)} %collective-permute-done.8.m2), channel_id=1, source_target_pairs={{0,1},{1,0},{2,3},{3,2},{4,5},{5,4},{6,7},{7,6},{8,9},{9,8},{10,11... | collective-permute-start | bytes 491528 | tf_op jit(solution)/shard_map/ppermute | solution.py:430
  109.4 2.4 %collective-permute-start.10 = (f32[2,640,128]{2,1,0:T(8,128)}, f32[2,640,128]{2,1,0:T(8,128)S(1)}, u32[]{:S(2)}, u32[]{:S(2)}) collective-permute-start(f32[2,640,128]{2,1,0:T(8,128)} %get-tuple-element.8), channel_id=1, source_target_pairs={{0,1},{1,0},{2,3},{3,2},{4,5},{5,4},{6,7},{7,6},{8,9},{9,8},{10,11... | collective-permute-start | bytes 1966088 | tf_op jit(solution)/shard_map/ppermute | solution.py:458
  111.8 20.2 %copy-start.6 = (bf16[640,128]{1,0:T(8,128)(2,1)S(1)}, bf16[640,128]{1,0:T(8,128)(2,1)}, u32[]{:S(2)}) copy-start(bf16[640,128]{1,0:T(8,128)(2,1)} %m0.1) | copy-start | bytes 491524
  111.8 20.2 %copy-start.13 = (f32[128]{0:T(128)S(1)}, f32[128]{0:T(128)}, u32[]{:S(2)}) copy-start(f32[128]{0:T(128)} %param.29) | copy-start | bytes 1540
  111.8 20.2 %copy-start.14 = (f32[128]{0:T(128)S(1)}, f32[128]{0:T(128)}, u32[]{:S(2)}) copy-start(f32[128]{0:T(128)} %param.28) | copy-start | bytes 1540
  113.0 11.3 %collective-permute-start.11 = (f32[640,128]{1,0:T(8,128)S(1)}, f32[640,128]{1,0:T(8,128)S(1)}, u32[]{:S(2)}, u32[]{:S(2)}) collective-permute-start(f32[640,128]{1,0:T(8,128)S(1)} %slice_bitcast_fusion), channel_id=1, source_target_pairs={{0,2},{1,3},{2,0},{3,1},{4,6},{5,7},{6,4},{7,5},{8,10},{9,11},{10,... | collective-permute-start | bytes 983048 | tf_op jit(solution)/shard_map/ppermute | solution.py:459

commit v2 on v1

v2 whole, which is shorter than its diff:
```python
import functools

import jax
import jax.numpy as jnp
from jax import lax
from jax.experimental import pallas as pl
from jax.experimental.pallas import tpu as pltpu
from jax.sharding import PartitionSpec as P


LAT = 640
HALO = 4
CHUNK = 512
SLOTS = 4
WINDOW = 7
PITCH = CHUNK + 8
UNROLL = 32
BUFFERS = 4

f32 = jnp.float32
bf16 = jnp.bfloat16


def silu(value):
    half = 0.5 * value
    return half + half * jnp.tanh(half)


def dot(left, right):
    return jnp.dot(left, right, preferred_element_type=f32)


def wide_row(ref, index):
    return ref[pl.ds(pl.multiple_of(index, 4), 4), :]


def chunk_of(tile):
    return jnp.concatenate([tile[j * PITCH : j * PITCH + CHUNK, :] for j in range(4)], axis=1)


def list_chunks(chunks, low_ref, high_ref, own_columns, outer, chunk_list):
    def step(i, count):
        halo = (low_ref[i] < HALO) | (high_ref[i] >= HALO + own_columns)
        mine = halo if outer else jnp.logical_not(halo)

        @pl.when(mine)
        def _():
            chunk_list[count] = i

        return count + jnp.where(mine, 1, 0)

    return lax.fori_loop(0, chunks, step, 0)


def list_columns(count, first_chunk, low_ref, high_ref, chunk_list, column_list, offset_list):
    slot0 = lax.shift_right_logical(first_chunk, 2)
    total = jnp.int32(0)
    seg_first = jnp.int32(1000)
    seg_last = jnp.int32(-1)
    seg_start = jnp.int32(0)
    for slot in range(SLOTS):

        def step(t, carry):
            low, high = carry
            i = chunk_list[t]
            here = lax.shift_right_logical(first_chunk + i, 2) == slot0 + slot
            return (
                jnp.where(here, jnp.minimum(low, low_ref[i]), low),
                jnp.where(here, jnp.maximum(high, high_ref[i]), high),
            )

        low, high = lax.fori_loop(0, count, step, (jnp.int32(1000), jnp.int32(-1)))
        has = high >= 0
        joins = has & (low >= seg_first) & (low <= seg_last + 1)
        begin = jnp.where(joins, seg_last + 1, low)
        fresh = jnp.where(has, jnp.maximum(high - begin + 1, 0), 0)
        base = total

        def put(j, carry):
            column_list[base + j] = begin + j
            return carry

        lax.fori_loop(0, fresh, put, 0)
        opens = has & jnp.logical_not(joins)
        seg_start = jnp.where(opens, total, seg_start)
        seg_first = jnp.where(opens, low, seg_first)
        seg_last = jnp.where(opens, high, jnp.maximum(seg_last, high))
        total = total + fresh
        offset_list[slot] = (seg_start - seg_first) * (LAT * 4)
    return total


def block_kernel(outer, chunks, own_columns, channels, nodes, *refs):
    place, points, receivers, low_ref, high_ref, grid = refs[:6]
    refs = refs[6:]
    if outer:
        low_own, low_swap, high_own, high_swap = refs[:4]
        refs = refs[4:]
    embed_in, embed_bias, ids, features = refs[:4]
    bundles = refs[4:8]
    meshes = refs[8:12]
    refs = refs[12:]
    if outer:
        message_bias, first_totals, first_tally, *parts = refs[:7]
        totals, tally = refs[-2:]
        refs = refs[7:-2]
    else:
        totals, tally = refs[:2]
        refs = refs[2:]
    (table, columns, sent, got, inputs, rows, embed_weight, send_weight, recv_weight,
     message_weight, mesh, extras, chunk_list, column_list, offset_list, in_sems, sems) = refs
    k = place[0]
    core = place[1]
    first_chunk = k * chunks
    count = list_chunks(chunks, low_ref, high_ref, own_columns, outer, chunk_list)
    total = list_columns(
        count, first_chunk, low_ref, high_ref, chunk_list, column_list, offset_list
    )

    copies = []
    for j in range(4):
        lanes = pl.ds(j * 128, 128)
        copies.append((bundles[j].at[pl.ds(0, 512)], send_weight.at[:, lanes]))
        copies.append((bundles[j].at[pl.ds(512, 512)], recv_weight.at[:, lanes]))
        copies.append((bundles[j].at[pl.ds(1536, 16)], extras.at[j]))
        at = pl.multiple_of(jnp.bitwise_xor(k, j) * 128, 128)
        copies.append((meshes[j], mesh.at[:, pl.ds(at, 128)]))
    copies = [pltpu.make_async_copy(a, b, sems.at[n]) for n, (a, b) in enumerate(copies)]
    late = []
    if outer:
        for j in range(4):
            for q in range(4):
                late.append(
                    pltpu.make_async_copy(
                        bundles[j].at[pl.ds(1024 + q * 128, 128)],
                        message_weight.at[pl.ds(j * 128, 128), pl.ds(q * 128, 128)],
                        sems.at[16 + j * 4 + q],
                    )
                )
        for copy in late:
            copy.start()
        totals[...] = first_totals[...]
        tally[...] = first_tally[...]
    else:
        totals[...] = jnp.zeros_like(totals)
        tally[...] = jnp.zeros_like(tally)

    def fetch(source, column, slot):
        start = pl.multiple_of(column * LAT, 128)
        pltpu.make_async_copy(
            source.at[:, pl.ds(start, LAT)], columns.at[slot], in_sems.at[slot]
        ).start()

    def start_column(i):
        column = column_list[i]
        slot = lax.rem(i, BUFFERS)
        if not outer:
            fetch(grid, column - HALO, slot)
            return
        inside = (column >= HALO) & (column < HALO + own_columns)

        @pl.when(inside)
        def _():
            fetch(grid, column - HALO, slot)

        for is_side, shift, direct, swapped in (
            (column < HALO, 0, low_own, low_swap),
            (column >= HALO + own_columns, HALO + own_columns, high_own, high_swap),
        ):
            place_in = column - shift
            half = lax.shift_right_arithmetic(place_in, 1)
            within = lax.bitwise_and(place_in, 1)

            @pl.when(is_side & (half == core))
            def _():
                fetch(direct, within, slot)

            @pl.when(is_side & (half != core))
            def _():
                fetch(swapped, within, slot)

    def turn(i, carry):
        slot = lax.rem(i, BUFFERS)

        @pl.when(i + BUFFERS - 1 < total)
        def _():
            start_column(i + BUFFERS - 1)

        pltpu.make_async_copy(
            grid.at[:, pl.ds(0, LAT)], columns.at[slot], in_sems.at[slot]
        ).wait()
        source = columns.at[slot]
        for l in range(LAT // 128):
            lanes = pl.ds(l * 128, 128)
            for j in range(4):
                top = min(channels, (j + 1) * 128)
                block = source[j * 128 : top, lanes]
                if top < (j + 1) * 128:
                    block = jnp.pad(block, ((0, (j + 1) * 128 - top), (0, 0)))
                row = pl.multiple_of((i * LAT + l * 128) * 4, 8)
                table[pl.ds(row + j, 128, stride=4), :] = block.T.astype(f32)
        return carry

    def sender_place(t):
        i = chunk_list[t]
        slot = lax.shift_right_logical(first_chunk + i, 2) - lax.shift_right_logical(
            first_chunk, 2
        )
        return i * CHUNK, offset_list[slot]

    @pl.when(count > 0)
    def _():
        for b in range(BUFFERS - 1):

            @pl.when(b < total)
            def _():
                start_column(b)

        for copy in copies:
            copy.start()
        embed_weight[464:512, :] = jnp.zeros((48, 512), bf16)
        embed_weight[0:channels, :] = embed_in[...]
        lax.fori_loop(0, total, turn, 0)
        for copy in copies:
            copy.wait()
        bias = jnp.concatenate(
            [
                sum(extras[j, 4 + r : 5 + r, :].astype(f32) for r in range(3))
                for j in range(4)
            ],
            axis=1,
        )
        terms = dot(mesh[...], recv_weight[...]) + bias
        for j in range(4):
            rows[pl.ds(j, nodes, stride=4), :] = terms[:, j * 128 : (j + 1) * 128]
        edge0, offset = sender_place(0)

        def gather(b, inner):
            base = edge0 + b * UNROLL
            for u in range(UNROLL):
                sent[pl.ds(b * UNROLL + u, 4, stride=PITCH), :] = wide_row(
                    table, points[base + u] + offset
                )
            return inner

        lax.fori_loop(0, CHUNK // UNROLL, gather, 0)
        features_by = jnp.concatenate([extras[j, 0:4, :] for j in range(4)], axis=1)

        def work(t, carry):
            i = chunk_list[t]
            edge = i * CHUNK
            inputs[...] = chunk_of(sent).astype(bf16)
            for e in range(CHUNK):
                got[pl.ds(e, 4, stride=PITCH), :] = wide_row(rows, receivers[edge + e])
            latent = silu(dot(inputs[...], embed_weight[...]) + embed_bias[...]).astype(bf16)
            before = (
                dot(latent, send_weight[...])
                + chunk_of(got)
                + lax.dot_general(
                    features[first_chunk + i], features_by, (((0,), (0,)), ((), ())),
                    preferred_element_type=f32,
                )
            )
            hidden = silu(before).astype(bf16)
            hot = jnp.where(
                lax.broadcasted_iota(jnp.int32, (nodes, CHUNK), 0) * 4 == ids[pl.ds(i, 1), :],
                1.0,
                0.0,
            )
            next_edge, next_offset = sender_place(jnp.minimum(t + 1, count - 1))
            for e in range(CHUNK):
                sent[pl.ds(e, 4, stride=PITCH), :] = wide_row(
                    table, points[next_edge + e] + next_offset
                )
            totals[...] += dot(hot.astype(bf16), hidden)
            tally[...] += (hot[:, 0:128] + hot[:, 128:256]) + (hot[:, 256:384] + hot[:, 384:512])
            return carry

        lax.fori_loop(0, count, work, 0)

    if not outer:
        return
    counts = jnp.sum(tally[...], axis=1, keepdims=True)
    whole = totals[...]
    upper = whole.astype(bf16)
    lower = (whole - upper.astype(f32)).astype(bf16)
    for copy in late:
        copy.wait()
    totals[...] = (
        dot(upper, message_weight[...])
        + dot(lower, message_weight[...])
        + counts * message_bias[...]
    )
    for r in range(2):
        mine = pl.multiple_of(jnp.bitwise_xor(k, 2 * r) * 128, 128)
        theirs = pl.multiple_of(jnp.bitwise_xor(k, 2 * r + 1) * 128, 128)
        parts[r][...] = totals[:, pl.ds(mine, 128)]
        parts[2 + r][...] = totals[:, pl.ds(theirs, 128)]


VMEM = pl.BlockSpec(memory_space=pltpu.VMEM)
SMEM = pl.BlockSpec(memory_space=pltpu.SMEM)
ANY = pl.BlockSpec(memory_space=pl.ANY)


def block_call(outer, chunks, own_columns, channels, nodes, operands):
    width = 512
    part = jax.ShapeDtypeStruct((nodes, 128), f32)
    sums = (
        jax.ShapeDtypeStruct((nodes, width), f32),
        jax.ShapeDtypeStruct((nodes, 128), f32),
    )
    specs = [SMEM] * 5 + [ANY] * (5 if outer else 1) + [VMEM] * 4 + [ANY] * 8
    if outer:
        specs = specs + [VMEM] * 3
    slots = SLOTS * WINDOW
    edges = chunks * CHUNK
    square = pltpu.VMEM((width, width), bf16)
    return pl.pallas_call(
        functools.partial(block_kernel, outer, chunks, own_columns, channels, nodes),
        out_shape=(part,) * 4 if outer else sums,
        in_specs=specs,
        out_specs=(VMEM,) * (4 if outer else 2),
        scratch_shapes=[
            pltpu.VMEM((slots * LAT * 4, 128), f32),
            pltpu.VMEM((BUFFERS, channels, LAT), bf16),
            pltpu.VMEM((4 * PITCH, 128), f32),
            pltpu.VMEM((4 * PITCH, 128), f32),
            pltpu.VMEM((CHUNK, width), bf16),
            pltpu.VMEM((nodes * 4, 128), f32),
            square,
            square,
            square,
            square,
            pltpu.VMEM((nodes, width), bf16),
            pltpu.VMEM((4, 16, 128), bf16),
            pltpu.SMEM((16,), jnp.int32),
            pltpu.SMEM((32,), jnp.int32),
            pltpu.SMEM((8,), jnp.int32),
            pltpu.SemaphoreType.DMA((BUFFERS,)),
            pltpu.SemaphoreType.DMA((32,)),
        ]
        + ([pltpu.VMEM(value.shape, f32) for value in sums] if outer else []),
        compiler_params=pltpu.CompilerParams(vmem_limit_bytes=60 * 2**20),
        cost_estimate=pl.CostEstimate(
            flops=2 * edges * width * (2 * width + nodes),
            bytes_accessed=2 * edges * width,
            transcendentals=2 * edges * width,
        ),
        name="block_outer" if outer else "block_inner",
    )(*operands)


def encoder(
    grid_inputs,
    embed_weight,
    embed_bias,
    mesh_latent,
    edge_features,
    senders,
    receivers,
    sender_weight,
    receiver_weight,
    feature_weight,
    hidden_bias,
    message_weight,
    message_bias,
    norm_gain,
    norm_shift,
):
    lon_count = lax.axis_size("lon")
    ch_count = lax.axis_size("ch")
    lon_place = lax.axis_index("lon")
    ch_place = lax.axis_index("ch")
    core = lax.bitwise_and(ch_place, 1)
    place = jnp.stack([ch_place, core]).astype(jnp.int32)
    points_own, channels = grid_inputs.shape
    own_columns = points_own // LAT
    mesh_nodes = mesh_latent.shape[0]
    full_width = message_weight.shape[1]
    edge_count = senders.shape[0]
    all_chunks = edge_count // CHUNK
    chunks = all_chunks // ch_count

    swap = [(i, i ^ 1) for i in range(ch_count)]
    across = [(i, i ^ 2) for i in range(ch_count)]
    facing = [
        (lon * ch_count + ch, (lon ^ 4) * ch_count + (ch ^ 2))
        for lon in range(lon_count)
        for ch in range(ch_count)
    ]
    forward = [(i, (i + 1) % lon_count) for i in range(lon_count)]
    backward = [(target, source) for source, target in forward]

    flat = grid_inputs.T
    half_points = HALO * LAT // 2
    low_half = lax.dynamic_slice_in_dim(
        flat, points_own - 2 * half_points + core * half_points, half_points, 1
    )
    high_half = lax.dynamic_slice_in_dim(flat, core * half_points, half_points, 1)
    low_own = lax.ppermute(low_half, "lon", forward)
    high_own = lax.ppermute(high_half, "lon", backward)
    low_swap = lax.ppermute(low_own, "ch", swap)
    high_swap = lax.ppermute(high_own, "ch", swap)

    part0 = lax.reduce_precision(hidden_bias, 8, 7)
    part1 = lax.reduce_precision(hidden_bias - part0, 8, 7)
    part2 = lax.reduce_precision(hidden_bias - part0 - part1, 8, 7)
    share = message_weight.shape[0]
    bundle = jnp.concatenate(
        [sender_weight, receiver_weight]
        + [message_weight[:, q * share : (q + 1) * share] for q in range(ch_count)]
        + [feature_weight, jnp.stack([part0, part1, part2]).astype(bf16)]
        + [jnp.zeros((9, share), bf16)],
        axis=0,
    )
    bundle_far = lax.ppermute(bundle, ("lon", "ch"), facing)
    bundle_near = lax.ppermute(bundle, "ch", swap)
    bundle_last = lax.ppermute(bundle_far, "ch", swap)
    mesh_far = lax.ppermute(mesh_latent, "ch", across)
    mesh_near = lax.ppermute(mesh_latent, "ch", swap)
    mesh_last = lax.ppermute(mesh_far, "ch", swap)

    own_senders, own_receivers = (
        lax.dynamic_slice_in_dim(ends.reshape(all_chunks, CHUNK), ch_place * chunks, chunks, 0)
        for ends in (senders, receivers)
    )
    points = jnp.mod(
        own_senders - lon_place * points_own + HALO * LAT, points_own * lon_count
    )
    low_column = jnp.min(points, axis=1) // LAT
    high_column = jnp.max(points, axis=1) // LAT
    ids = (own_receivers - lon_place * mesh_nodes) * 4
    feature_blocks = jnp.transpose(
        edge_features.reshape(edge_features.shape[0], all_chunks, CHUNK), (1, 0, 2)
    )

    call = functools.partial(
        block_call, chunks=chunks, own_columns=own_columns, channels=channels, nodes=mesh_nodes
    )
    scalars = [place, (points * 4).reshape(-1), ids.reshape(-1), low_column, high_column, flat]
    arrays = [
        embed_weight, embed_bias[None, :], ids, feature_blocks,
        bundle, bundle_near, bundle_far, bundle_last,
        mesh_latent, mesh_near, mesh_far, mesh_last,
    ]
    totals, tally = call(False, operands=scalars + arrays)
    keep_here, keep_far, send_here, send_far = call(
        True,
        operands=scalars
        + [low_own, low_swap, high_own, high_swap]
        + arrays
        + [message_bias[None, :], totals, tally],
    )
    far = keep_far + lax.ppermute(send_far, "ch", swap)
    far = lax.ppermute(far.astype(bf16), "ch", across).astype(f32)
    node_share = keep_here + lax.ppermute(send_here, "ch", swap) + far
    first_sum, second = lax.psum(
        (
            jnp.sum(node_share, axis=1, keepdims=True),
            jnp.sum(jnp.square(node_share), axis=1, keepdims=True),
        ),
        "ch",
    )
    centre = first_sum / full_width
    spread = second / full_width - jnp.square(centre)
    normed = (node_share - centre) * lax.rsqrt(spread + 1.0)
    return (mesh_latent.astype(f32) + normed * norm_gain + norm_shift).astype(bf16)


def solution(mesh):
    return jax.shard_map(
        encoder,
        mesh=mesh,
        in_specs=(
            P("lon", None),
            P(),
            P(),
            P("lon", "ch"),
            P(None, "lon"),
            P("lon"),
            P("lon"),
            P(None, "ch"),
            P(None, "ch"),
            P(None, "ch"),
            P("ch"),
            P("ch", None),
            P(),
            P("ch"),
            P("ch"),
        ),
        out_specs=P("lon", "ch"),
        check_vma=False,
    )
```

time: 134 us -> 114 us (0.85)
  Pallas kernels: 61.7 us -> 42.1 us
  waiting for transfers between devices: 45.6 us -> 40.8 us
  starting transfers between devices: 6.94 us -> 10.7 us
    pallas_call x3 -> x2, Pallas kernels: 61.7 us -> 42.1 us  [block_call(): pl.pallas_call(functools.partial(block_kernel, outer, chunks, own_columns...]
    ppermute x12 -> x13, waiting for transfers between devices: 45.6 us -> 40.8 us  [the longest x1 30.4 us: encoder(): mesh_far = lax.ppermute(mesh_latent, 'ch', across)]
    ppermute x12 -> x13, starting transfers between devices: 6.94 us -> 10.7 us  [the longest x1 3.99 us: encoder(): bundle_far = lax.ppermute(bundle, ('lon', 'ch'), facing)]
    reshape x2 -> x4, local copies, waits for them, and re-layouts: 0.67 us -> 3.03 us  [the longest x2 1.81 us: encoder(): ends.reshape(all_chunks, CHUNK)]
    pad x1 -> x0, local copies, waits for them, and re-layouts: 1.87 us -> none  [on_device(): weight = jnp.pad(embed_weight, ((0, full_width - channels), (0, 0)))]
  transfers between devices with their start and end apart: 12 -> 13, of which waited for: 5 -> 4; matrix products, arithmetic and copies ran while one was open for 4% -> 5% of each run, Pallas kernels for 27% -> 24%
where the time goes in v2:
time: 114 us; the launch traced here: 113 us
  Pallas kernels  42.1 us (37%)
  waiting for transfers between devices  40.8 us (36%)
  starting transfers between devices  10.7 us (9%)
  blocking collectives  7.34 us (6%)
  local copies, waits for them, and re-layouts  6.73 us (6%)
  other arithmetic  4.83 us (4%)
    pallas_call x2, Pallas kernels, block_call(): pl.pallas_call(functools.partial(block_kernel, outer, chunks, own_columns...  42.1 us
    ppermute x1, waiting for transfers between devices, encoder(): mesh_far = lax.ppermute(mesh_latent, 'ch', across)  30.4 us
    ppermute x1, waiting for transfers between devices, encoder(): far = lax.ppermute(far.astype(bf16), 'ch', across).astype(f32)  7.6 us
    psum x1, blocking collectives, encoder(): lax.psum((jnp.sum(node_share, axis=1, keepdims=True), jnp.sum(jnp.square(...  7.34 us
    ppermute x1, starting transfers between devices, encoder(): bundle_far = lax.ppermute(bundle, ('lon', 'ch'), facing)  3.99 us
    dynamic_slice x1, local copies, waits for them, and re-layouts, encoder(): lax.dynamic_slice_in_dim(flat, core * half_points, half_points, 1)  3.34 us
    ppermute x1, starting transfers between devices, encoder(): low_own = lax.ppermute(low_half, 'lon', forward)  3.31 us
  transfers between devices with their start and end apart: 13, of which 4 were waited for; matrix products, arithmetic and copies ran while one was open for 5% of the time, Pallas kernels for 24%

profile of v2, /device:TPU:6, one launch (start us, length us, event | category | flops | bytes accessed | tf_op | source)
XLA Modules:
  0.0 112.8 jit_solution(1001169267076658420)
XLA Ops:
  0.0 0.0 copy-start.11
  0.0 0.0 copy-start.9
  0.0 0.0 copy-start.10
  0.0 0.0 copy-start.3
  0.0 3.3 %dynamic-slice_bitcast_fusion = (bf16[474,1280]{1,0:T(8,128)(2,1)}, bf16[474,1280]{1,0:T(8,128)(2,1)}) fusion(bf16[28800,474]{0,1:T(8,128)(2,1)} %param.15, s32[]{:T(128)S(6)} %select_n.30, s32[]{:T(128)S(6)} %select_n.29), kind=kLoop, calls=%fused_computation | loop fusion | bytes 4853768 | tf_op jit(solution)/shard_map/dynamic_slice | solution.py:400
  3.4 0.8 collective-permute-start.2
  4.2 3.3 %collective-permute-start = (bf16[474,1280]{1,0:T(8,128)(2,1)}, bf16[474,1280]{1,0:T(8,128)(2,1)S(1)}, u32[]{:S(2)}, u32[]{:S(2)}) collective-permute-start(bf16[474,1280]{1,0:T(8,128)(2,1)} %get-tuple-element.27), channel_id=1, source_target_pairs={{0,4},{4,8},{8,12},{12,16},{16,20},{20,24},{24,28},{28,32},{32,36}... | collective-permute-start | bytes 3640328 | tf_op jit(solution)/shard_map/ppermute | solution.py:401
  7.5 0.0 copy-done.11
  7.5 0.0 copy-done.7
  7.6 0.0 copy-done.8
  7.6 0.0 copy-done.9
  7.6 0.0 copy-done.10
  7.6 0.3 concatenate.4.refs_10_.refs_14_
  7.9 0.0 copy-start
  7.9 4.0 %collective-permute-start.5 = (bf16[1552,128]{1,0:T(8,128)(2,1)S(1)}, bf16[1552,128]{1,0:T(8,128)(2,1)S(1)}, u32[]{:S(2)}, u32[]{:S(2)}) collective-permute-start(bf16[1552,128]{1,0:T(8,128)(2,1)S(1)} %concatenate.4.refs_10_.refs_14_), channel_id=1, source_target_pairs={{0,18},{1,19},{2,16},{3,17},{4,22},{5,23},{6,20},{7,21},{8,26},{9,... | collective-permute-start | bytes 1191944 | tf_op jit(solution)/shard_map/ppermute | solution.py:417
  11.9 0.0 copy-done.3
  11.9 0.6 collective-permute-start.8
  12.5 0.0 collective-permute-start.7
  12.5 0.9 reshape.17
  13.4 0.2 fusion.5
  13.6 30.4 %collective-permute-done.8.refs_16_.refs_20_ = bf16[640,128]{1,0:T(8,128)(2,1)} collective-permute-done((bf16[640,128]{1,0:T(8,128)(2,1)S(1)}, bf16[640,128]{1,0:T(8,128)(2,1)}, u32[]{:S(2)}, u32[]{:S(2)}) %collective-permute-start.8) | collective-permute-done | bytes 163872 | tf_op jit(solution)/shard_map/ppermute | solution.py:420
  44.0 0.0 collective-permute-start.4
  44.0 0.0 collective-permute-done.5.refs_12_.refs_16_
  44.0 0.5 collective-permute-start.6
  44.5 0.0 collective-permute-done.2.refs_8_
  44.5 0.1 collective-permute-start.3
  44.6 0.0 collective-permute-done.refs_6_
  44.6 0.4 collective-permute-start.1
  45.0 0.8 and_select_fusion
  45.9 0.9 reshape.19
  46.8 0.0 collective-permute-done.7.refs_15_.refs_19_
  46.8 0.1 collective-permute-start.9
  46.9 0.0 copy-start.6
  46.9 0.6 reshape.18.refs_1_
  47.5 0.6 reshape.20.refs_2_
  48.2 0.6 pad_add_fusion.refs_0_
  48.8 1.4 %collective-permute-done.9.refs_17_.refs_21_ = bf16[640,128]{1,0:T(8,128)(2,1)} collective-permute-done((bf16[640,128]{1,0:T(8,128)(2,1)}, bf16[640,128]{1,0:T(8,128)(2,1)}, u32[]{:S(2)}, u32[]{:S(2)}) %collective-permute-start.9) | collective-permute-done | bytes 163872 | tf_op jit(solution)/shard_map/ppermute | solution.py:422
  50.2 0.0 collective-permute-done.4.refs_11_.refs_15_
  50.2 0.0 collective-permute-done.6.refs_13_.refs_17_
  50.2 0.0 copy-done
  50.2 0.0 copy-done.5
  50.2 0.0 copy-done.6
  50.2 26.7 %block_inner.1 = (f32[640,512]{1,0:T(8,128)}, f32[640,128]{1,0:T(8,128)}) custom-call(s32[2]{0:T(128)} %pad_add_fusion.refs_0_, s32[5632]{0:T(1024)} %reshape.18.refs_1_, s32[5632]{0:T(1024)} %reshape.20.refs_2_, s32[11]{0:T(128)} %get-tuple-element.37.refs_3_, s32[11]{0:T(128)} %get-tuple-element.36.refs_4_, bf16[474,28800]{1,0:T(8,128)(2,1)} %bitcast.18, ...), custom_call_target="tpu_custom_call" | custom-call | flops 9596567552 | bytes 5767168 | tf_op jit(solution)/shard_map/block_inner/pallas_call | solution.py:319
  76.9 0.0 copy-done.1
  77.0 0.0 copy-done.2
  77.0 0.0 collective-permute-done.3.refs_9_
  77.0 0.0 collective-permute-done.1.refs_7_
  77.0 15.4 %block_outer.1 = (f32[640,128]{1,0:T(8,128)}, f32[640,128]{1,0:T(8,128)}, f32[640,128]{1,0:T(8,128)}, f32[640,128]{1,0:T(8,128)}) custom-call(s32[2]{0:T(128)} %pad_add_fusion.refs_0_, s32[5632]{0:T(1024)} %reshape.18.refs_1_, s32[5632]{0:T(1024)} %reshape.20.refs_2_, s32[11]{0:T(128)} %get-tuple-element.37.refs_3_, s32[11]{0:T(128)} %get-tuple-element.36.refs_4_, ...), custom_call_target="tpu_custom_call" | custom-call | flops 9596567552 | bytes 5767168 | tf_op jit(solution)/shard_map/block_outer/pallas_call | solution.py:319
  92.4 0.0 copy-start.4
  92.4 0.0 copy-start.12
  92.4 0.0 copy-start.13
  92.4 0.1 collective-permute-start.11
  92.5 0.5 collective-permute-start.10
  93.0 1.3 %collective-permute-done.11 = f32[640,128]{1,0:T(8,128)S(1)} collective-permute-done((f32[640,128]{1,0:T(8,128)}, f32[640,128]{1,0:T(8,128)S(1)}, u32[]{:S(2)}, u32[]{:S(2)}) %collective-permute-start.11) | collective-permute-done | bytes 327712 | tf_op jit(solution)/shard_map/ppermute | solution.py:455
  94.3 1.0 add_convert_fusion.1
  95.3 0.2 collective-permute-start.12
  95.6 0.0 collective-permute-done.10
  95.6 7.6 %collective-permute-done.12 = bf16[640,128]{1,0:T(8,128)(2,1)S(1)} collective-permute-done((bf16[640,128]{1,0:T(8,128)(2,1)S(1)}, bf16[640,128]{1,0:T(8,128)(2,1)S(1)}, u32[]{:S(2)}, u32[]{:S(2)}) %collective-permute-start.12) | collective-permute-done | bytes 163872 | tf_op jit(solution)/shard_map/ppermute | solution.py:456
  103.2 1.2 %fusion.7 = (f32[640]{0:T(1024)S(1)}, f32[640]{0:T(1024)S(1)}, f32[640,128]{1,0:T(8,128)S(1)}) fusion(bf16[640,128]{1,0:T(8,128)(2,1)S(1)} %collective-permute-done.12, f32[640,128]{1,0:T(8,128)} %get-tuple-element.13, f32[640,128]{1,0:T(8,128)S(1)} %collective-permute-done.10), kind=kLoop, calls=%fused_computation.26 | loop fusion | flops 490240 | bytes 1152000 | tf_op jit(solution)/shard_map/reduce_sum | solution.py:460
  104.4 7.3 %all-reduce = (f32[640,1]{0,1:T(1,128)S(1)}, f32[640,1]{0,1:T(1,128)S(1)}) all-reduce(f32[640,1]{0,1:T(1,128)S(1)} %broadcast_in_dim.20, f32[640,1]{0,1:T(1,128)S(1)} %broadcast_in_dim.21), channel_id=1, replica_groups=mesh['lon'=32,'ch'=4] {'ch'}, use_global_device_ids=true, to_apply=%region_3.4 | all-reduce | flops 1280 | bytes 10240 | tf_op jit(solution)/shard_map/psum | solution.py:458
  111.8 0.0 copy-done.4
  111.8 0.0 copy-done.12
  111.8 0.0 copy-done.13
  111.8 0.9 add_convert_fusion
  (12 shorter events, 0.1 us)
Async XLA Ops:
  0.0 7.5 %copy-start.11 = (f32[128]{0:T(128)S(1)}, f32[128]{0:T(128)}, u32[]{:S(2)}) copy-start(f32[128]{0:T(128)} %param.25) | copy-start | bytes 1540
  0.0 7.5 %copy-start.7 = (bf16[128,512]{1,0:T(8,128)(2,1)S(1)}, bf16[128,512]{1,0:T(8,128)(2,1)}, u32[]{:S(2)}) copy-start(bf16[128,512]{1,0:T(8,128)(2,1)} %param.26) | copy-start | bytes 393220
  0.0 7.6 %copy-start.8 = (bf16[512,128]{1,0:T(8,128)(2,1)S(1)}, bf16[512,128]{1,0:T(8,128)(2,1)}, u32[]{:S(2)}) copy-start(bf16[512,128]{1,0:T(8,128)(2,1)} %param.22) | copy-start | bytes 393220
  0.0 7.6 %copy-start.9 = (bf16[512,128]{1,0:T(8,128)(2,1)S(1)}, bf16[512,128]{1,0:T(8,128)(2,1)}, u32[]{:S(2)}) copy-start(bf16[512,128]{1,0:T(8,128)(2,1)} %param.23) | copy-start | bytes 393220
  0.0 7.6 %copy-start.10 = (bf16[4,128]{1,0:T(4,128)(2,1)S(1)}, bf16[4,128]{1,0:T(4,128)(2,1)}, u32[]{:S(2)}) copy-start(bf16[4,128]{1,0:T(4,128)(2,1)} %param.24) | copy-start | bytes 3076
  0.0 11.8 %copy-start.3 = (bf16[640,128]{1,0:T(8,128)(2,1)S(1)}, bf16[640,128]{1,0:T(8,128)(2,1)}, u32[]{:S(2)}) copy-start(bf16[640,128]{1,0:T(8,128)(2,1)} %refs_18_.1) | copy-start | bytes 491524
  3.4 41.1 %collective-permute-start.2 = (bf16[474,1280]{1,0:T(8,128)(2,1)}, bf16[474,1280]{1,0:T(8,128)(2,1)S(1)}, u32[]{:S(2)}, u32[]{:S(2)}) collective-permute-start(bf16[474,1280]{1,0:T(8,128)(2,1)} %get-tuple-element.26), channel_id=1, source_target_pairs={{4,0},{8,4},{12,8},{16,12},{20,16},{24,20},{28,24},{32,28},{36,32}... | collective-permute-start | bytes 3640328 | tf_op jit(solution)/shard_map/ppermute | solution.py:402
  4.2 40.4 %collective-permute-start = (bf16[474,1280]{1,0:T(8,128)(2,1)}, bf16[474,1280]{1,0:T(8,128)(2,1)S(1)}, u32[]{:S(2)}, u32[]{:S(2)}) collective-permute-start(bf16[474,1280]{1,0:T(8,128)(2,1)} %get-tuple-element.27), channel_id=1, source_target_pairs={{0,4},{4,8},{8,12},{12,16},{16,20},{20,24},{24,28},{28,32},{32,36}... | collective-permute-start | bytes 3640328 | tf_op jit(solution)/shard_map/ppermute | solution.py:401
  7.9 42.3 %copy-start = (bf16[1552,128]{1,0:T(8,128)(2,1)}, bf16[1552,128]{1,0:T(8,128)(2,1)S(1)}, u32[]{:S(2)}) copy-start(bf16[1552,128]{1,0:T(8,128)(2,1)S(1)} %concatenate.4.refs_10_.refs_14_) | copy-start | bytes 1191940
  7.9 36.1 %collective-permute-start.5 = (bf16[1552,128]{1,0:T(8,128)(2,1)S(1)}, bf16[1552,128]{1,0:T(8,128)(2,1)S(1)}, u32[]{:S(2)}, u32[]{:S(2)}) collective-permute-start(bf16[1552,128]{1,0:T(8,128)(2,1)S(1)} %concatenate.4.refs_10_.refs_14_), channel_id=1, source_target_pairs={{0,18},{1,19},{2,16},{3,17},{4,22},{5,23},{6,20},{7,21},{8,26},{9,... | collective-permute-start | bytes 1191944 | tf_op jit(solution)/shard_map/ppermute | solution.py:417
  11.9 32.1 %collective-permute-start.8 = (bf16[640,128]{1,0:T(8,128)(2,1)S(1)}, bf16[640,128]{1,0:T(8,128)(2,1)}, u32[]{:S(2)}, u32[]{:S(2)}) collective-permute-start(bf16[640,128]{1,0:T(8,128)(2,1)S(1)} %copy-done.3), channel_id=1, source_target_pairs={{0,2},{1,3},{2,0},{3,1},{4,6},{5,7},{6,4},{7,5},{8,10},{9,11},{10,... | collective-permute-start | bytes 491528 | tf_op jit(solution)/shard_map/ppermute | solution.py:420
  12.5 34.3 %collective-permute-start.7 = (bf16[640,128]{1,0:T(8,128)(2,1)S(1)}, bf16[640,128]{1,0:T(8,128)(2,1)}, u32[]{:S(2)}, u32[]{:S(2)}) collective-permute-start(bf16[640,128]{1,0:T(8,128)(2,1)S(1)} %copy-done.3), channel_id=1, source_target_pairs={{0,1},{1,0},{2,3},{3,2},{4,5},{5,4},{6,7},{7,6},{8,9},{9,8},{10,11... | collective-permute-start | bytes 491528 | tf_op jit(solution)/shard_map/ppermute | solution.py:421
  44.0 6.2 %collective-permute-start.4 = (bf16[1552,128]{1,0:T(8,128)(2,1)S(1)}, bf16[1552,128]{1,0:T(8,128)(2,1)}, u32[]{:S(2)}, u32[]{:S(2)}) collective-permute-start(bf16[1552,128]{1,0:T(8,128)(2,1)S(1)} %concatenate.4.refs_10_.refs_14_), channel_id=1, source_target_pairs={{0,1},{1,0},{2,3},{3,2},{4,5},{5,4},{6,7},{7,6},{8,9},{9,8},{10,11... | collective-permute-start | bytes 1191944 | tf_op jit(solution)/shard_map/ppermute | solution.py:418
  44.0 6.2 %copy-start.5 = (bf16[1552,128]{1,0:T(8,128)(2,1)}, bf16[1552,128]{1,0:T(8,128)(2,1)S(1)}, u32[]{:S(2)}) copy-start(bf16[1552,128]{1,0:T(8,128)(2,1)S(1)} %collective-permute-done.5.refs_12_.refs_16_) | copy-start | bytes 1191940
  44.0 6.2 %collective-permute-start.6 = (bf16[1552,128]{1,0:T(8,128)(2,1)S(1)}, bf16[1552,128]{1,0:T(8,128)(2,1)}, u32[]{:S(2)}, u32[]{:S(2)}) collective-permute-start(bf16[1552,128]{1,0:T(8,128)(2,1)S(1)} %collective-permute-done.5.refs_12_.refs_16_), channel_id=1, source_target_pairs={{0,1},{1,0},{2,3},{3,2},{4,5},{5,4},{6,7},{7,6},{8,9},{9,8},{10,11... | collective-permute-start | bytes 1191944 | tf_op jit(solution)/shard_map/ppermute | solution.py:419
  44.5 32.4 %copy-start.1 = (bf16[474,1280]{1,0:T(8,128)(2,1)}, bf16[474,1280]{1,0:T(8,128)(2,1)S(1)}, u32[]{:S(2)}) copy-start(bf16[474,1280]{1,0:T(8,128)(2,1)S(1)} %collective-permute-done.2.refs_8_) | copy-start | bytes 3640324
  44.5 32.4 %collective-permute-start.3 = (bf16[474,1280]{1,0:T(8,128)(2,1)S(1)}, bf16[474,1280]{1,0:T(8,128)(2,1)}, u32[]{:S(2)}, u32[]{:S(2)}) collective-permute-start(bf16[474,1280]{1,0:T(8,128)(2,1)S(1)} %collective-permute-done.2.refs_8_), channel_id=1, source_target_pairs={{0,1},{1,0},{2,3},{3,2},{4,5},{5,4},{6,7},{7,6},{8,9},{9,8},{10,11... | collective-permute-start | bytes 3640328 | tf_op jit(solution)/shard_map/ppermute | solution.py:404
  44.6 32.3 %copy-start.2 = (bf16[474,1280]{1,0:T(8,128)(2,1)}, bf16[474,1280]{1,0:T(8,128)(2,1)S(1)}, u32[]{:S(2)}) copy-start(bf16[474,1280]{1,0:T(8,128)(2,1)S(1)} %collective-permute-done.refs_6_) | copy-start | bytes 3640324
  44.6 32.3 %collective-permute-start.1 = (bf16[474,1280]{1,0:T(8,128)(2,1)S(1)}, bf16[474,1280]{1,0:T(8,128)(2,1)}, u32[]{:S(2)}, u32[]{:S(2)}) collective-permute-start(bf16[474,1280]{1,0:T(8,128)(2,1)S(1)} %collective-permute-done.refs_6_), channel_id=1, source_target_pairs={{0,1},{1,0},{2,3},{3,2},{4,5},{5,4},{6,7},{7,6},{8,9},{9,8},{10,11... | collective-permute-start | bytes 3640328 | tf_op jit(solution)/shard_map/ppermute | solution.py:403
  46.8 3.4 %collective-permute-start.9 = (bf16[640,128]{1,0:T(8,128)(2,1)}, bf16[640,128]{1,0:T(8,128)(2,1)}, u32[]{:S(2)}, u32[]{:S(2)}) collective-permute-start(bf16[640,128]{1,0:T(8,128)(2,1)} %collective-permute-done.8.refs_16_.refs_20_), channel_id=1, source_target_pairs={{0,1},{1,0},{2,3},{3,2},{4,5},{5,4},{6,7},{7,6},{8,9},{9,8},{10,11... | collective-permute-start | bytes 491528 | tf_op jit(solution)/shard_map/ppermute | solution.py:422
  46.9 3.3 %copy-start.6 = (s32[11,512]{1,0:T(8,128)}, s32[11,512]{1,0:T(8,128)S(1)}, u32[]{:S(2)}) copy-start(s32[11,512]{1,0:T(8,128)S(1)} %subtract_multiply_fusion.refs_8_.refs_12_) | copy-start | bytes 67588
  92.4 19.5 %copy-start.4 = (bf16[640,128]{1,0:T(8,128)(2,1)S(1)}, bf16[640,128]{1,0:T(8,128)(2,1)}, u32[]{:S(2)}) copy-start(bf16[640,128]{1,0:T(8,128)(2,1)} %refs_18_.1) | copy-start | bytes 491524
  92.4 19.5 %copy-start.12 = (f32[128]{0:T(128)S(1)}, f32[128]{0:T(128)}, u32[]{:S(2)}) copy-start(f32[128]{0:T(128)} %param.29) | copy-start | bytes 1540
  92.4 19.5 %copy-start.13 = (f32[128]{0:T(128)S(1)}, f32[128]{0:T(128)}, u32[]{:S(2)}) copy-start(f32[128]{0:T(128)} %param.28) | copy-start | bytes 1540
  92.4 1.9 %collective-permute-start.11 = (f32[640,128]{1,0:T(8,128)}, f32[640,128]{1,0:T(8,128)S(1)}, u32[]{:S(2)}, u32[]{:S(2)}) collective-permute-start(f32[640,128]{1,0:T(8,128)} %get-tuple-element.16), channel_id=1, source_target_pairs={{0,1},{1,0},{2,3},{3,2},{4,5},{5,4},{6,7},{7,6},{8,9},{9,8},{10,11... | collective-permute-start | bytes 983048 | tf_op jit(solution)/shard_map/ppermute | solution.py:455
  92.5 3.1 %collective-permute-start.10 = (f32[640,128]{1,0:T(8,128)}, f32[640,128]{1,0:T(8,128)S(1)}, u32[]{:S(2)}, u32[]{:S(2)}) collective-permute-start(f32[640,128]{1,0:T(8,128)} %get-tuple-element.14), channel_id=1, source_target_pairs={{0,1},{1,0},{2,3},{3,2},{4,5},{5,4},{6,7},{7,6},{8,9},{9,8},{10,11... | collective-permute-start | bytes 983048 | tf_op jit(solution)/shard_map/ppermute | solution.py:457
  95.3 7.8 %collective-permute-start.12 = (bf16[640,128]{1,0:T(8,128)(2,1)S(1)}, bf16[640,128]{1,0:T(8,128)(2,1)S(1)}, u32[]{:S(2)}, u32[]{:S(2)}) collective-permute-start(bf16[640,128]{1,0:T(8,128)(2,1)S(1)} %add_convert_fusion.1), channel_id=1, source_target_pairs={{0,2},{1,3},{2,0},{3,1},{4,6},{5,7},{6,4},{7,5},{8,10},{9,11},{10,... | collective-permute-start | bytes 491528 | tf_op jit(solution)/shard_map/ppermute | solution.py:456

commit v3 on v2

--- a/solution.py
+++ b/solution.py
@@ -16,6 +16,7 @@
 PITCH = CHUNK + 8
 UNROLL = 32
 BUFFERS = 4
+LIMIT = 6
 
 f32 = jnp.float32
 bf16 = jnp.bfloat16
@@ -39,17 +40,19 @@
 
 
 def list_chunks(chunks, low_ref, high_ref, own_columns, outer, chunk_list):
-    def step(i, count):
+    def step(i, counts):
+        inner_count, outer_count = counts
         halo = (low_ref[i] < HALO) | (high_ref[i] >= HALO + own_columns)
-        mine = halo if outer else jnp.logical_not(halo)
-
-        @pl.when(mine)
+        early = jnp.logical_not(halo) & (inner_count < LIMIT)
+        count = outer_count if outer else inner_count
+
+        @pl.when(jnp.logical_not(early) if outer else early)
         def _():
             chunk_list[count] = i
 
-        return count + jnp.where(mine, 1, 0)
-
-    return lax.fori_loop(0, chunks, step, 0)
+        return inner_count + jnp.where(early, 1, 0), outer_count + jnp.where(early, 0, 1)
+
+    return lax.fori_loop(0, chunks, step, (jnp.int32(0), jnp.int32(0)))[1 if outer else 0]
 
 
 def list_columns(count, first_chunk, low_ref, high_ref, chunk_list, column_list, offset_list):
@@ -110,7 +113,7 @@
     (table, columns, sent, got, inputs, rows, embed_weight, send_weight, recv_weight,
      message_weight, mesh, extras, chunk_list, column_list, offset_list, in_sems, sems) = refs
     k = place[0]
-    core = place[1]
+    core = lax.bitwise_and(k, 1)
     first_chunk = k * chunks
     count = list_chunks(chunks, low_ref, high_ref, own_columns, outer, chunk_list)
     total = list_columns(
@@ -262,18 +265,18 @@
                 )
             )
             hidden = silu(before).astype(bf16)
-            hot = jnp.where(
-                lax.broadcasted_iota(jnp.int32, (nodes, CHUNK), 0) * 4 == ids[pl.ds(i, 1), :],
-                1.0,
-                0.0,
-            )
+            node = lax.broadcasted_iota(jnp.int32, (nodes, 128), 0) * 4
+            hots = [
+                jnp.where(node == ids[pl.ds(i * 4 + q, 1), :], 1.0, 0.0) for q in range(4)
+            ]
+            hot = jnp.concatenate([value.astype(bf16) for value in hots], axis=1)
             next_edge, next_offset = sender_place(jnp.minimum(t + 1, count - 1))
             for e in range(CHUNK):
                 sent[pl.ds(e, 4, stride=PITCH), :] = wide_row(
                     table, points[next_edge + e] + next_offset
                 )
-            totals[...] += dot(hot.astype(bf16), hidden)
-            tally[...] += (hot[:, 0:128] + hot[:, 128:256]) + (hot[:, 256:384] + hot[:, 384:512])
+            totals[...] += dot(hot, hidden)
+            tally[...] += (hots[0] + hots[1]) + (hots[2] + hots[3])
             return carry
 
         lax.fori_loop(0, count, work, 0)
@@ -296,6 +299,73 @@
         theirs = pl.multiple_of(jnp.bitwise_xor(k, 2 * r + 1) * 128, 128)
         parts[r][...] = totals[:, pl.ds(mine, 128)]
         parts[2 + r][...] = totals[:, pl.ds(theirs, 128)]
+
+
+def pack_kernel(chunks, points_own, all_points, nodes, share, place, senders, receivers,
+                feature_weight, hidden_bias, grid, sender_weight, receiver_weight, message_weight,
+                points, ids, low_ref, high_ref, bundle, low_half, high_half, extra, sems):
+    lon = place[0]
+    k = place[1]
+    half = HALO * LAT // 2
+    side = lax.bitwise_and(k, 1) * half
+    low_at = pl.multiple_of(points_own - 2 * half + side, 128)
+    copies = [
+        (sender_weight, bundle.at[pl.ds(0, 512)]),
+        (receiver_weight, bundle.at[pl.ds(512, 512)]),
+        (grid.at[:, pl.ds(low_at, half)], low_half),
+        (grid.at[:, pl.ds(pl.multiple_of(side, 128), half)], high_half),
+    ]
+    for q in range(4):
+        copies.append(
+            (
+                message_weight.at[:, pl.ds(q * share, share)],
+                bundle.at[pl.ds(1024 + q * share, share)],
+            )
+        )
+    copies = [pltpu.make_async_copy(a, b, sems.at[n]) for n, (a, b) in enumerate(copies)]
+    for copy in copies:
+        copy.start()
+    bias = hidden_bias[...]
+    upper = bias.astype(bf16)
+    middle = (bias - upper.astype(f32)).astype(bf16)
+    lower = (bias - upper.astype(f32) - middle.astype(f32)).astype(bf16)
+    extra[...] = jnp.concatenate(
+        [feature_weight[...].astype(f32)]
+        + [value.astype(f32) for value in (upper, middle, lower)]
+        + [jnp.zeros((9, share), f32)],
+        axis=0,
+    ).astype(bf16)
+    last = pltpu.make_async_copy(extra, bundle.at[pl.ds(1536, 16)], sems.at[len(copies)])
+    last.start()
+    for i in range(chunks):
+        rows = pl.ds(pl.multiple_of((k * chunks + i) * 4, 4), 4)
+        point = senders[rows, :] - lon * points_own + HALO * LAT
+        point = jnp.where(point < 0, point + all_points, point)
+        point = jnp.where(point >= all_points, point - all_points, point)
+        points[i * 4 : i * 4 + 4, :] = point * 4
+        ids[i * 4 : i * 4 + 4, :] = (receivers[rows, :] - lon * nodes) * 4
+        for ref, end in ((low_ref, jnp.min(point)), (high_ref, jnp.max(point))):
+            ref[i] = lax.shift_right_logical(lax.shift_right_logical(end, 7) * 13108, 16)
+    for copy in copies:
+        copy.wait()
+    last.wait()
+
+
+def pack_call(chunks, points_own, all_points, channels, nodes, share, operands):
+    half = HALO * LAT // 2
+    index = jax.ShapeDtypeStruct((chunks * 4, 128), jnp.int32)
+    ends = jax.ShapeDtypeStruct((chunks,), jnp.int32)
+    side = jax.ShapeDtypeStruct((channels, half), bf16)
+    return pl.pallas_call(
+        functools.partial(pack_kernel, chunks, points_own, all_points, nodes, share),
+        out_shape=(
+            index, index, ends, ends, jax.ShapeDtypeStruct((1552, share), bf16), side, side,
+        ),
+        in_specs=[SMEM] + [VMEM] * 4 + [ANY] * 4,
+        out_specs=(VMEM, VMEM, SMEM, SMEM, ANY, ANY, ANY),
+        scratch_shapes=[pltpu.VMEM((16, share), bf16), pltpu.SemaphoreType.DMA((9,))],
+        name="pack",
+    )(*operands)
 
 
 VMEM = pl.BlockSpec(memory_space=pltpu.VMEM)
@@ -372,8 +442,7 @@
     ch_count = lax.axis_size("ch")
     lon_place = lax.axis_index("lon")
     ch_place = lax.axis_index("ch")
-    core = lax.bitwise_and(ch_place, 1)
-    place = jnp.stack([ch_place, core]).astype(jnp.int32)
+    place = ch_place[None].astype(jnp.int32)
     points_own, channels = grid_inputs.shape
     own_columns = points_own // LAT
     mesh_nodes = mesh_latent.shape[0]
@@ -393,44 +462,31 @@
     backward = [(target, source) for source, target in forward]
 
     flat = grid_inputs.T
-    half_points = HALO * LAT // 2
-    low_half = lax.dynamic_slice_in_dim(
-        flat, points_own - 2 * half_points + core * half_points, half_points, 1
-    )
-    high_half = lax.dynamic_slice_in_dim(flat, core * half_points, half_points, 1)
+    points, ids, low_column, high_column, bundle, low_half, high_half = pack_call(
+        chunks, points_own, points_own * lon_count, channels, mesh_nodes,
+        message_weight.shape[0],
+        [
+            jnp.stack([lon_place, ch_place]).astype(jnp.int32),
+            senders.reshape(-1, 128),
+            receivers.reshape(-1, 128),
+            feature_weight,
+            hidden_bias[None, :],
+            flat,
+            sender_weight,
+            receiver_weight,
+            message_weight,
+        ],
+    )
+    mesh_far = lax.ppermute(mesh_latent, "ch", across)
+    bundle_far = lax.ppermute(bundle, ("lon", "ch"), facing)
     low_own = lax.ppermute(low_half, "lon", forward)
     high_own = lax.ppermute(high_half, "lon", backward)
     low_swap = lax.ppermute(low_own, "ch", swap)
     high_swap = lax.ppermute(high_own, "ch", swap)
-
-    part0 = lax.reduce_precision(hidden_bias, 8, 7)
-    part1 = lax.reduce_precision(hidden_bias - part0, 8, 7)
-    part2 = lax.reduce_precision(hidden_bias - part0 - part1, 8, 7)
-    share = message_weight.shape[0]
-    bundle = jnp.concatenate(
-        [sender_weight, receiver_weight]
-        + [message_weight[:, q * share : (q + 1) * share] for q in range(ch_count)]
-        + [feature_weight, jnp.stack([part0, part1, part2]).astype(bf16)]
-        + [jnp.zeros((9, share), bf16)],
-        axis=0,
-    )
-    bundle_far = lax.ppermute(bundle, ("lon", "ch"), facing)
     bundle_near = lax.ppermute(bundle, "ch", swap)
     bundle_last = lax.ppermute(bundle_far, "ch", swap)
-    mesh_far = lax.ppermute(mesh_latent, "ch", across)
     mesh_near = lax.ppermute(mesh_latent, "ch", swap)
     mesh_last = lax.ppermute(mesh_far, "ch", swap)
-
-    own_senders, own_receivers = (
-        lax.dynamic_slice_in_dim(ends.reshape(all_chunks, CHUNK), ch_place * chunks, chunks, 0)
-        for ends in (senders, receivers)
-    )
-    points = jnp.mod(
-        own_senders - lon_place * points_own + HALO * LAT, points_own * lon_count
-    )
-    low_column = jnp.min(points, axis=1) // LAT
-    high_column = jnp.max(points, axis=1) // LAT
-    ids = (own_receivers - lon_place * mesh_nodes) * 4
     feature_blocks = jnp.transpose(
         edge_features.reshape(edge_features.shape[0], all_chunks, CHUNK), (1, 0, 2)
     )
@@ -438,7 +494,7 @@
     call = functools.partial(
         block_call, chunks=chunks, own_columns=own_columns, channels=channels, nodes=mesh_nodes
     )
-    scalars = [place, (points * 4).reshape(-1), ids.reshape(-1), low_column, high_column, flat]
+    scalars = [place, points.reshape(-1), ids.reshape(-1), low_column, high_column, flat]
     arrays = [
         embed_weight, embed_bias[None, :], ids, feature_blocks,
         bundle, bundle_near, bundle_far, bundle_last,

time: 114 us -> 200 us (1.75)
  Pallas kernels: 42.1 us -> 132 us
  waiting for transfers between devices: 40.8 us -> 46 us
  local copies, waits for them, and re-layouts: 6.73 us -> 2.59 us
  starting transfers between devices: 10.7 us -> 7.21 us
    pallas_call x0 -> x1, Pallas kernels: none -> 89.2 us  [pack_call(): pl.pallas_call(functools.partial(pack_kernel, chunks, points_own, all_poi...]
    ppermute x1, waiting for transfers between devices: 0.01 us -> 10.9 us  [encoder(): bundle_far = lax.ppermute(bundle, ('lon', 'ch'), facing)]
    ppermute x1, waiting for transfers between devices: 30.4 us -> 21.7 us  [encoder(): mesh_far = lax.ppermute(mesh_latent, 'ch', across)]
    dynamic_slice x1 -> x0, local copies, waits for them, and re-layouts: 3.34 us -> none  [encoder(): lax.dynamic_slice_in_dim(flat, core * half_points, half_points, 1)]
    reshape x4 -> x0, local copies, waits for them, and re-layouts: 3.03 us -> none  [the longest x2 1.81 us: encoder(): ends.reshape(all_chunks, CHUNK)]
    unnamed x28 -> x26, local copies, waits for them, and re-layouts: 0.07 us -> 2.58 us
    ppermute x1, waiting for transfers between devices: 1.42 us -> 3.6 us  [encoder(): mesh_last = lax.ppermute(mesh_far, 'ch', swap)]
  transfers between devices with their start and end apart: 13 -> 13, of which waited for: 4 -> 6; matrix products, arithmetic and copies ran while one was open for 5% -> 1% of each run, Pallas kernels for 24% -> 11%
where the time goes in v3:
time: 200 us; the launch traced here: 199 us
  Pallas kernels  132 us (66%)
  waiting for transfers between devices  46 us (23%)
  blocking collectives  7.34 us (4%)
  starting transfers between devices  7.21 us (4%)
  other arithmetic  3.81 us (2%)
  local copies, waits for them, and re-layouts  2.59 us (1%)
    pallas_call x1, Pallas kernels, pack_call(): pl.pallas_call(functools.partial(pack_kernel, chunks, points_own, all_poi...  89.2 us
    pallas_call x2, Pallas kernels, block_call(): pl.pallas_call(functools.partial(block_kernel, outer, chunks, own_columns...  43 us
    ppermute x1, waiting for transfers between devices, encoder(): mesh_far = lax.ppermute(mesh_latent, 'ch', across)  21.7 us
    ppermute x1, waiting for transfers between devices, encoder(): bundle_far = lax.ppermute(bundle, ('lon', 'ch'), facing)  10.9 us
    ppermute x1, waiting for transfers between devices, encoder(): far = lax.ppermute(far.astype(bf16), 'ch', across).astype(f32)  7.68 us
    psum x1, blocking collectives, encoder(): lax.psum((jnp.sum(node_share, axis=1, keepdims=True), jnp.sum(jnp.square(...  7.34 us
  transfers between devices with their start and end apart: 13, of which 6 were waited for; matrix products, arithmetic and copies ran while one was open for 1% of the time, Pallas kernels for 11%

profile of v3, /device:TPU:6, one launch (start us, length us, event | category | flops | bytes accessed | tf_op | source)
XLA Modules:
  0.0 199.3 jit_solution(3027252203063919269)
XLA Ops:
  0.0 0.6 pad_add_fusion.place
  0.6 0.0 copy-start.3
  0.6 89.2 %pack.1 = (s32[44,128]{1,0:T(8,128)}, s32[44,128]{1,0:T(8,128)}, s32[11]{0:T(128)}, s32[11]{0:T(128)}, bf16[1552,128]{1,0:T(8,128)(2,1)}, /*index=5*/bf16[474,1280]{1,0:T(8,128)(2,1)}, bf16[474,1280]{1,0:T(8,128)(2,1)}) custom-call(s32[2]{0:T(128)} %pad_add_fusion.place, s32[176,128]{1,0:T(8,128)} %bitcast.20, s32[176,128]{1,0:T(8,128)} %bitcast.21, ...), custom_call_target="tpu_custom_call" | custom-call | tf_op jit(solution)/shard_map/pack/pallas_call | solution.py:359
  89.8 1.6 collective-permute-start
  91.3 0.5 collective-permute-start.2
  91.9 3.0 %collective-permute-start.5 = (bf16[1552,128]{1,0:T(8,128)(2,1)}, bf16[1552,128]{1,0:T(8,128)(2,1)S(1)}, u32[]{:S(2)}, u32[]{:S(2)}) collective-permute-start(bf16[1552,128]{1,0:T(8,128)(2,1)} %get-tuple-element.24.refs_10_.refs_14_), channel_id=1, source_target_pairs={{0,18},{1,19},{2,16},{3,17},{4,22},{5,23},{6,20},{7,21},{8,26},{9,... | collective-permute-start | bytes 1191944 | tf_op jit(solution)/shard_map/ppermute | solution.py:481
  94.9 0.0 copy-done.3
  94.9 0.6 collective-permute-start.8
  95.5 0.0 collective-permute-start.4
  95.5 10.9 %collective-permute-done.5.refs_12_.refs_16_ = bf16[1552,128]{1,0:T(8,128)(2,1)S(1)} collective-permute-done((bf16[1552,128]{1,0:T(8,128)(2,1)}, bf16[1552,128]{1,0:T(8,128)(2,1)S(1)}, u32[]{:S(2)}, u32[]{:S(2)}) %collective-permute-start.5) | collective-permute-done | bytes 397344 | tf_op jit(solution)/shard_map/ppermute | solution.py:481
  106.4 0.0 copy-start.5
  106.4 0.0 collective-permute-start.6
  106.4 21.7 %collective-permute-done.8.refs_16_.refs_20_ = bf16[640,128]{1,0:T(8,128)(2,1)S(1)} collective-permute-done((bf16[640,128]{1,0:T(8,128)(2,1)S(1)}, bf16[640,128]{1,0:T(8,128)(2,1)S(1)}, u32[]{:S(2)}, u32[]{:S(2)}) %collective-permute-start.8) | collective-permute-done | bytes 163872 | tf_op jit(solution)/shard_map/ppermute | solution.py:480
  128.1 0.0 copy-start.8
  128.1 0.0 collective-permute-start.7
  128.1 0.0 collective-permute-done.refs_6_
  128.2 0.0 copy-start
  128.2 0.5 collective-permute-start.1
  128.7 0.0 collective-permute-done.2.refs_8_
  128.7 0.0 copy-start.1
  128.7 0.1 collective-permute-start.3
  128.8 0.8 collective-permute-done.7.refs_15_.refs_19_
  129.5 0.0 copy-done.5
  129.5 0.0 copy-start.9
  129.5 0.1 collective-permute-start.9
  129.7 3.6 %collective-permute-done.9.refs_17_.refs_21_ = bf16[640,128]{1,0:T(8,128)(2,1)S(1)} collective-permute-done((bf16[640,128]{1,0:T(8,128)(2,1)S(1)}, bf16[640,128]{1,0:T(8,128)(2,1)S(1)}, u32[]{:S(2)}, u32[]{:S(2)}) %collective-permute-start.9) | collective-permute-done | bytes 163872 | tf_op jit(solution)/shard_map/ppermute | solution.py:489
  133.3 0.0 copy-start.10
  133.3 0.0 collective-permute-done.4.refs_11_.refs_15_
  133.3 0.0 copy-start.6
  133.3 0.0 collective-permute-done.6.refs_13_.refs_17_
  133.3 0.8 copy-done.6
  134.1 0.0 copy-start.7
  134.1 0.7 copy-done.7
  134.8 0.0 copy-done.9
  134.8 0.0 copy-done.8
  134.8 0.0 copy-done.10
  134.8 22.0 %block_inner.1 = (f32[640,512]{1,0:T(8,128)}, f32[640,128]{1,0:T(8,128)}) custom-call(s32[1]{0:T(128)} %bitcast.refs_0_, s32[5632]{0:T(1024)} %bitcast.22, s32[5632]{0:T(1024)} %bitcast.18, s32[11]{0:T(128)} %get-tuple-element.20.refs_3_, s32[11]{0:T(128)} %get-tuple-element.21.refs_4_, bf16[474,28800]{1,0:T(8,128)(2,1)} %bitcast.14, ...), custom_call_target="tpu_custom_call" | custom-call | flops 9596567552 | bytes 5767168 | tf_op jit(solution)/shard_map/block_inner/pallas_call | solution.py:389
  156.8 0.0 copy-done
  156.8 0.0 copy-done.1
  156.8 0.0 collective-permute-done.1.refs_7_
  156.8 0.0 copy-start.2
  156.8 0.0 collective-permute-done.3.refs_9_
  156.9 1.0 copy-done.2
  157.9 21.0 %block_outer.1 = (f32[640,128]{1,0:T(8,128)}, f32[640,128]{1,0:T(8,128)}, f32[640,128]{1,0:T(8,128)}, f32[640,128]{1,0:T(8,128)}) custom-call(s32[1]{0:T(128)} %bitcast.refs_0_, s32[5632]{0:T(1024)} %bitcast.23, s32[5632]{0:T(1024)} %bitcast.19, s32[11]{0:T(128)} %get-tuple-element.20.refs_3_, s32[11]{0:T(128)} %get-tuple-element.21.refs_4_, ...), custom_call_target="tpu_custom_call" | custom-call | flops 9596567552 | bytes 5767168 | tf_op jit(solution)/shard_map/block_outer/pallas_call | solution.py:389
  178.9 0.0 copy-start.4
  178.9 0.0 copy-start.11
  178.9 0.0 copy-start.12
  178.9 0.1 collective-permute-start.11
  179.0 0.5 collective-permute-start.10
  179.5 1.3 collective-permute-done.11
  180.9 1.0 add_convert_fusion.1
  181.9 0.1 collective-permute-start.12
  182.0 0.0 collective-permute-done.10
  182.0 7.7 %collective-permute-done.12 = bf16[640,128]{1,0:T(8,128)(2,1)S(1)} collective-permute-done((bf16[640,128]{1,0:T(8,128)(2,1)S(1)}, bf16[640,128]{1,0:T(8,128)(2,1)S(1)}, u32[]{:S(2)}, u32[]{:S(2)}) %collective-permute-start.12) | collective-permute-done | bytes 163872 | tf_op jit(solution)/shard_map/ppermute | solution.py:512
  189.7 1.2 fusion
  191.0 7.3 %all-reduce = (f32[640,1]{0,1:T(1,128)S(1)}, f32[640,1]{0,1:T(1,128)S(1)}) all-reduce(f32[640,1]{0,1:T(1,128)S(1)} %broadcast_in_dim.24, f32[640,1]{0,1:T(1,128)S(1)} %broadcast_in_dim.25), channel_id=1, replica_groups=mesh['lon'=32,'ch'=4] {'ch'}, use_global_device_ids=true, to_apply=%region_1.0 | all-reduce | flops 1280 | bytes 10240 | tf_op jit(solution)/shard_map/psum | solution.py:514
  198.4 0.0 copy-done.4
  198.4 0.0 copy-done.11
  198.4 0.0 copy-done.12
  198.4 0.9 add_convert_fusion
  (3 shorter events, 0.0 us)
Async XLA Ops:
  0.6 94.3 %copy-start.3 = (bf16[640,128]{1,0:T(8,128)(2,1)S(1)}, bf16[640,128]{1,0:T(8,128)(2,1)}, u32[]{:S(2)}) copy-start(bf16[640,128]{1,0:T(8,128)(2,1)} %refs_18_.1) | copy-start | bytes 491524
  89.8 38.4 %collective-permute-start = (bf16[474,1280]{1,0:T(8,128)(2,1)}, bf16[474,1280]{1,0:T(8,128)(2,1)S(1)}, u32[]{:S(2)}, u32[]{:S(2)}) collective-permute-start(bf16[474,1280]{1,0:T(8,128)(2,1)} %get-tuple-element.22), channel_id=1, source_target_pairs={{0,4},{4,8},{8,12},{12,16},{16,20},{20,24},{24,28},{28,32},{32,36}... | collective-permute-start | bytes 3640328 | tf_op jit(solution)/shard_map/ppermute | solution.py:482
  91.3 37.3 %collective-permute-start.2 = (bf16[474,1280]{1,0:T(8,128)(2,1)}, bf16[474,1280]{1,0:T(8,128)(2,1)S(1)}, u32[]{:S(2)}, u32[]{:S(2)}) collective-permute-start(bf16[474,1280]{1,0:T(8,128)(2,1)} %get-tuple-element.23), channel_id=1, source_target_pairs={{4,0},{8,4},{12,8},{16,12},{20,16},{24,20},{28,24},{32,28},{36,32}... | collective-permute-start | bytes 3640328 | tf_op jit(solution)/shard_map/ppermute | solution.py:483
  91.9 14.5 %collective-permute-start.5 = (bf16[1552,128]{1,0:T(8,128)(2,1)}, bf16[1552,128]{1,0:T(8,128)(2,1)S(1)}, u32[]{:S(2)}, u32[]{:S(2)}) collective-permute-start(bf16[1552,128]{1,0:T(8,128)(2,1)} %get-tuple-element.24.refs_10_.refs_14_), channel_id=1, source_target_pairs={{0,18},{1,19},{2,16},{3,17},{4,22},{5,23},{6,20},{7,21},{8,26},{9,... | collective-permute-start | bytes 1191944 | tf_op jit(solution)/shard_map/ppermute | solution.py:481
  94.9 33.3 %collective-permute-start.8 = (bf16[640,128]{1,0:T(8,128)(2,1)S(1)}, bf16[640,128]{1,0:T(8,128)(2,1)S(1)}, u32[]{:S(2)}, u32[]{:S(2)}) collective-permute-start(bf16[640,128]{1,0:T(8,128)(2,1)S(1)} %copy-done.3), channel_id=1, source_target_pairs={{0,2},{1,3},{2,0},{3,1},{4,6},{5,7},{6,4},{7,5},{8,10},{9,11},{10,... | collective-permute-start | bytes 491528 | tf_op jit(solution)/shard_map/ppermute | solution.py:480
  95.5 37.8 %collective-permute-start.4 = (bf16[1552,128]{1,0:T(8,128)(2,1)}, bf16[1552,128]{1,0:T(8,128)(2,1)S(1)}, u32[]{:S(2)}, u32[]{:S(2)}) collective-permute-start(bf16[1552,128]{1,0:T(8,128)(2,1)} %get-tuple-element.24.refs_10_.refs_14_), channel_id=1, source_target_pairs={{0,1},{1,0},{2,3},{3,2},{4,5},{5,4},{6,7},{7,6},{8,9},{9,8},{10,11... | collective-permute-start | bytes 1191944 | tf_op jit(solution)/shard_map/ppermute | solution.py:486
  106.4 23.1 %copy-start.5 = (bf16[1552,128]{1,0:T(8,128)(2,1)}, bf16[1552,128]{1,0:T(8,128)(2,1)S(1)}, u32[]{:S(2)}) copy-start(bf16[1552,128]{1,0:T(8,128)(2,1)S(1)} %collective-permute-done.5.refs_12_.refs_16_) | copy-start | bytes 1191940
  106.4 26.9 %collective-permute-start.6 = (bf16[1552,128]{1,0:T(8,128)(2,1)S(1)}, bf16[1552,128]{1,0:T(8,128)(2,1)S(1)}, u32[]{:S(2)}, u32[]{:S(2)}) collective-permute-start(bf16[1552,128]{1,0:T(8,128)(2,1)S(1)} %collective-permute-done.5.refs_12_.refs_16_), channel_id=1, source_target_pairs={{0,1},{1,0},{2,3},{3,2},{4,5},{5,4},{6,7},{7,6},{8,9},{9,8},{10,11... | collective-permute-start | bytes 1191944 | tf_op jit(solution)/shard_map/ppermute | solution.py:487
  128.1 6.7 %copy-start.8 = (bf16[640,128]{1,0:T(8,128)(2,1)}, bf16[640,128]{1,0:T(8,128)(2,1)S(1)}, u32[]{:S(2)}) copy-start(bf16[640,128]{1,0:T(8,128)(2,1)S(1)} %collective-permute-done.8.refs_16_.refs_20_) | copy-start | bytes 491524
  128.1 1.4 collective-permute-start.7
  128.2 28.7 %copy-start = (bf16[474,1280]{1,0:T(8,128)(2,1)}, bf16[474,1280]{1,0:T(8,128)(2,1)S(1)}, u32[]{:S(2)}) copy-start(bf16[474,1280]{1,0:T(8,128)(2,1)S(1)} %collective-permute-done.refs_6_) | copy-start | bytes 3640324
  128.2 28.7 %collective-permute-start.1 = (bf16[474,1280]{1,0:T(8,128)(2,1)S(1)}, bf16[474,1280]{1,0:T(8,128)(2,1)S(1)}, u32[]{:S(2)}, u32[]{:S(2)}) collective-permute-start(bf16[474,1280]{1,0:T(8,128)(2,1)S(1)} %collective-permute-done.refs_6_), channel_id=1, source_target_pairs={{0,1},{1,0},{2,3},{3,2},{4,5},{5,4},{6,7},{7,6},{8,9},{9,8},{10,11... | collective-permute-start | bytes 3640328 | tf_op jit(solution)/shard_map/ppermute | solution.py:484
  128.7 28.2 %copy-start.1 = (bf16[474,1280]{1,0:T(8,128)(2,1)}, bf16[474,1280]{1,0:T(8,128)(2,1)S(1)}, u32[]{:S(2)}) copy-start(bf16[474,1280]{1,0:T(8,128)(2,1)S(1)} %collective-permute-done.2.refs_8_) | copy-start | bytes 3640324
  128.7 28.2 %collective-permute-start.3 = (bf16[474,1280]{1,0:T(8,128)(2,1)S(1)}, bf16[474,1280]{1,0:T(8,128)(2,1)}, u32[]{:S(2)}, u32[]{:S(2)}) collective-permute-start(bf16[474,1280]{1,0:T(8,128)(2,1)S(1)} %collective-permute-done.2.refs_8_), channel_id=1, source_target_pairs={{0,1},{1,0},{2,3},{3,2},{4,5},{5,4},{6,7},{7,6},{8,9},{9,8},{10,11... | collective-permute-start | bytes 3640328 | tf_op jit(solution)/shard_map/ppermute | solution.py:485
  129.5 5.3 %copy-start.9 = (bf16[640,128]{1,0:T(8,128)(2,1)}, bf16[640,128]{1,0:T(8,128)(2,1)S(1)}, u32[]{:S(2)}) copy-start(bf16[640,128]{1,0:T(8,128)(2,1)S(1)} %collective-permute-done.7.refs_15_.refs_19_) | copy-start | bytes 491524
  129.5 3.7 %collective-permute-start.9 = (bf16[640,128]{1,0:T(8,128)(2,1)S(1)}, bf16[640,128]{1,0:T(8,128)(2,1)S(1)}, u32[]{:S(2)}, u32[]{:S(2)}) collective-permute-start(bf16[640,128]{1,0:T(8,128)(2,1)S(1)} %collective-permute-done.8.refs_16_.refs_20_), channel_id=1, source_target_pairs={{0,1},{1,0},{2,3},{3,2},{4,5},{5,4},{6,7},{7,6},{8,9},{9,8},{10,11... | collective-permute-start | bytes 491528 | tf_op jit(solution)/shard_map/ppermute | solution.py:489
  133.3 1.5 copy-start.10
  133.3 0.8 copy-start.6
  134.1 0.7 copy-start.7
  156.8 1.0 copy-start.2
  178.9 19.5 %copy-start.4 = (bf16[640,128]{1,0:T(8,128)(2,1)S(1)}, bf16[640,128]{1,0:T(8,128)(2,1)}, u32[]{:S(2)}) copy-start(bf16[640,128]{1,0:T(8,128)(2,1)} %refs_18_.1) | copy-start | bytes 491524
  178.9 19.5 %copy-start.11 = (f32[128]{0:T(128)S(1)}, f32[128]{0:T(128)}, u32[]{:S(2)}) copy-start(f32[128]{0:T(128)} %param.29) | copy-start | bytes 1540
  178.9 19.5 %copy-start.12 = (f32[128]{0:T(128)S(1)}, f32[128]{0:T(128)}, u32[]{:S(2)}) copy-start(f32[128]{0:T(128)} %param.28) | copy-start | bytes 1540
  178.9 1.9 collective-permute-start.11
  179.0 3.0 %collective-permute-start.10 = (f32[640,128]{1,0:T(8,128)}, f32[640,128]{1,0:T(8,128)S(1)}, u32[]{:S(2)}, u32[]{:S(2)}) collective-permute-start(f32[640,128]{1,0:T(8,128)} %get-tuple-element.28), channel_id=1, source_target_pairs={{0,1},{1,0},{2,3},{3,2},{4,5},{5,4},{6,7},{7,6},{8,9},{9,8},{10,11... | collective-permute-start | bytes 983048 | tf_op jit(solution)/shard_map/ppermute | solution.py:513
  181.9 7.8 %collective-permute-start.12 = (bf16[640,128]{1,0:T(8,128)(2,1)S(1)}, bf16[640,128]{1,0:T(8,128)(2,1)S(1)}, u32[]{:S(2)}, u32[]{:S(2)}) collective-permute-start(bf16[640,128]{1,0:T(8,128)(2,1)S(1)} %add_convert_fusion.1), channel_id=1, source_target_pairs={{0,2},{1,3},{2,0},{3,1},{4,6},{5,7},{6,4},{7,5},{8,10},{9,11},{10,... | collective-permute-start | bytes 491528 | tf_op jit(solution)/shard_map/ppermute | solution.py:512

commit v4 on v3

--- a/solution.py
+++ b/solution.py
@@ -104,6 +104,8 @@
     meshes = refs[8:12]
     refs = refs[12:]
     if outer:
+        messages = refs[:4]
+        refs = refs[4:]
         message_bias, first_totals, first_tally, *parts = refs[:7]
         totals, tally = refs[-2:]
         refs = refs[7:-2]
@@ -125,21 +127,18 @@
         lanes = pl.ds(j * 128, 128)
         copies.append((bundles[j].at[pl.ds(0, 512)], send_weight.at[:, lanes]))
         copies.append((bundles[j].at[pl.ds(512, 512)], recv_weight.at[:, lanes]))
-        copies.append((bundles[j].at[pl.ds(1536, 16)], extras.at[j]))
+        copies.append((bundles[j].at[pl.ds(1024, 16)], extras.at[j]))
         at = pl.multiple_of(jnp.bitwise_xor(k, j) * 128, 128)
         copies.append((meshes[j], mesh.at[:, pl.ds(at, 128)]))
     copies = [pltpu.make_async_copy(a, b, sems.at[n]) for n, (a, b) in enumerate(copies)]
     late = []
     if outer:
         for j in range(4):
-            for q in range(4):
-                late.append(
-                    pltpu.make_async_copy(
-                        bundles[j].at[pl.ds(1024 + q * 128, 128)],
-                        message_weight.at[pl.ds(j * 128, 128), pl.ds(q * 128, 128)],
-                        sems.at[16 + j * 4 + q],
-                    )
+            late.append(
+                pltpu.make_async_copy(
+                    messages[j], message_weight.at[pl.ds(j * 128, 128)], sems.at[16 + j]
                 )
+            )
         for copy in late:
             copy.start()
         totals[...] = first_totals[...]
@@ -301,42 +300,36 @@
         parts[2 + r][...] = totals[:, pl.ds(theirs, 128)]
 
 
-def pack_kernel(chunks, points_own, all_points, nodes, share, place, senders, receivers,
-                feature_weight, hidden_bias, grid, sender_weight, receiver_weight, message_weight,
-                points, ids, low_ref, high_ref, bundle, low_half, high_half, extra, sems):
+def weights_kernel(place, feature_weight, hidden_bias, sender_weight, receiver_weight, bundle):
+    bundle[0:512, :] = sender_weight[...]
+    bundle[512:1024, :] = receiver_weight[...]
+    bias = hidden_bias[...]
+    upper = bias.astype(bf16)
+    middle = (bias - upper.astype(f32)).astype(bf16)
+    lower = (bias - upper.astype(f32) - middle.astype(f32)).astype(bf16)
+    bundle[1024:1040, :] = jnp.concatenate(
+        [feature_weight[...].astype(f32)]
+        + [value.astype(f32) for value in (upper, middle, lower)]
+        + [jnp.zeros((9, bias.shape[1]), f32)],
+        axis=0,
+    ).astype(bf16)
+
+
+def pack_kernel(chunks, points_own, all_points, nodes, place, senders, receivers, grid,
+                points, ids, low_ref, high_ref, low_half, high_half, sems):
     lon = place[0]
     k = place[1]
     half = HALO * LAT // 2
     side = lax.bitwise_and(k, 1) * half
     low_at = pl.multiple_of(points_own - 2 * half + side, 128)
     copies = [
-        (sender_weight, bundle.at[pl.ds(0, 512)]),
-        (receiver_weight, bundle.at[pl.ds(512, 512)]),
-        (grid.at[:, pl.ds(low_at, half)], low_half),
-        (grid.at[:, pl.ds(pl.multiple_of(side, 128), half)], high_half),
+        pltpu.make_async_copy(grid.at[:, pl.ds(low_at, half)], low_half, sems.at[0]),
+        pltpu.make_async_copy(
+            grid.at[:, pl.ds(pl.multiple_of(side, 128), half)], high_half, sems.at[1]
+        ),
     ]
-    for q in range(4):
-        copies.append(
-            (
-                message_weight.at[:, pl.ds(q * share, share)],
-                bundle.at[pl.ds(1024 + q * share, share)],
-            )
-        )
-    copies = [pltpu.make_async_copy(a, b, sems.at[n]) for n, (a, b) in enumerate(copies)]
     for copy in copies:
         copy.start()
-    bias = hidden_bias[...]
-    upper = bias.astype(bf16)
-    middle = (bias - upper.astype(f32)).astype(bf16)
-    lower = (bias - upper.astype(f32) - middle.astype(f32)).astype(bf16)
-    extra[...] = jnp.concatenate(
-        [feature_weight[...].astype(f32)]
-        + [value.astype(f32) for value in (upper, middle, lower)]
-        + [jnp.zeros((9, share), f32)],
-        axis=0,
-    ).astype(bf16)
-    last = pltpu.make_async_copy(extra, bundle.at[pl.ds(1536, 16)], sems.at[len(copies)])
-    last.start()
     for i in range(chunks):
         rows = pl.ds(pl.multiple_of((k * chunks + i) * 4, 4), 4)
         point = senders[rows, :] - lon * points_own + HALO * LAT
@@ -348,22 +341,29 @@
             ref[i] = lax.shift_right_logical(lax.shift_right_logical(end, 7) * 13108, 16)
     for copy in copies:
         copy.wait()
-    last.wait()
-
-
-def pack_call(chunks, points_own, all_points, channels, nodes, share, operands):
+
+
+def weights_call(share, operands):
+    return pl.pallas_call(
+        weights_kernel,
+        out_shape=jax.ShapeDtypeStruct((1040, share), bf16),
+        in_specs=[SMEM] + [VMEM] * 4,
+        out_specs=VMEM,
+        name="weights",
+    )(*operands)
+
+
+def pack_call(chunks, points_own, all_points, channels, nodes, operands):
     half = HALO * LAT // 2
     index = jax.ShapeDtypeStruct((chunks * 4, 128), jnp.int32)
     ends = jax.ShapeDtypeStruct((chunks,), jnp.int32)
     side = jax.ShapeDtypeStruct((channels, half), bf16)
     return pl.pallas_call(
-        functools.partial(pack_kernel, chunks, points_own, all_points, nodes, share),
-        out_shape=(
-            index, index, ends, ends, jax.ShapeDtypeStruct((1552, share), bf16), side, side,
-        ),
-        in_specs=[SMEM] + [VMEM] * 4 + [ANY] * 4,
-        out_specs=(VMEM, VMEM, SMEM, SMEM, ANY, ANY, ANY),
-        scratch_shapes=[pltpu.VMEM((16, share), bf16), pltpu.SemaphoreType.DMA((9,))],
+        functools.partial(pack_kernel, chunks, points_own, all_points, nodes),
+        out_shape=(index, index, ends, ends, side, side),
+        in_specs=[SMEM] + [VMEM] * 2 + [ANY],
+        out_specs=(VMEM, VMEM, SMEM, SMEM, VMEM, VMEM),
+        scratch_shapes=[pltpu.SemaphoreType.DMA((2,))],
         name="pack",
     )(*operands)
 
@@ -382,7 +382,7 @@
     )
     specs = [SMEM] * 5 + [ANY] * (5 if outer else 1) + [VMEM] * 4 + [ANY] * 8
     if outer:
-        specs = specs + [VMEM] * 3
+        specs = specs + [ANY] * 4 + [VMEM] * 3
     slots = SLOTS * WINDOW
     edges = chunks * CHUNK
     square = pltpu.VMEM((width, width), bf16)
@@ -462,23 +462,17 @@
     backward = [(target, source) for source, target in forward]
 
     flat = grid_inputs.T
-    points, ids, low_column, high_column, bundle, low_half, high_half = pack_call(
+    place_all = jnp.stack([lon_place, ch_place]).astype(jnp.int32)
+    bundle = weights_call(
+        message_weight.shape[0],
+        [place_all, feature_weight, hidden_bias[None, :], sender_weight, receiver_weight],
+    )
+    bundle_far = lax.ppermute(bundle, ("lon", "ch"), facing)
+    mesh_far = lax.ppermute(mesh_latent, "ch", across)
+    points, ids, low_column, high_column, low_half, high_half = pack_call(
         chunks, points_own, points_own * lon_count, channels, mesh_nodes,
-        message_weight.shape[0],
-        [
-            jnp.stack([lon_place, ch_place]).astype(jnp.int32),
-            senders.reshape(-1, 128),
-            receivers.reshape(-1, 128),
-            feature_weight,
-            hidden_bias[None, :],
-            flat,
-            sender_weight,
-            receiver_weight,
-            message_weight,
-        ],
-    )
-    mesh_far = lax.ppermute(mesh_latent, "ch", across)
-    bundle_far = lax.ppermute(bundle, ("lon", "ch"), facing)
+        [place_all, senders.reshape(-1, 128), receivers.reshape(-1, 128), flat],
+    )
     low_own = lax.ppermute(low_half, "lon", forward)
     high_own = lax.ppermute(high_half, "lon", backward)
     low_swap = lax.ppermute(low_own, "ch", swap)
@@ -487,6 +481,9 @@
     bundle_last = lax.ppermute(bundle_far, "ch", swap)
     mesh_near = lax.ppermute(mesh_latent, "ch", swap)
     mesh_last = lax.ppermute(mesh_far, "ch", swap)
+    message_far = lax.ppermute(message_weight, ("lon", "ch"), facing)
+    message_near = lax.ppermute(message_weight, "ch", swap)
+    message_last = lax.ppermute(message_far, "ch", swap)
     feature_blocks = jnp.transpose(
         edge_features.reshape(edge_features.shape[0], all_chunks, CHUNK), (1, 0, 2)
     )
@@ -506,6 +503,7 @@
         operands=scalars
         + [low_own, low_swap, high_own, high_swap]
         + arrays
+        + [message_weight, message_near, message_far, message_last]
         + [message_bias[None, :], totals, tally],
     )
     far = keep_far + lax.ppermute(send_far, "ch", swap)

time: 200 us -> 112 us (0.56)
  Pallas kernels: 132 us -> 48.8 us
  waiting for transfers between devices: 46 us -> 41.2 us
  starting transfers between devices: 7.21 us -> 9.47 us
    pallas_call x1, Pallas kernels: 89.2 us -> 4.13 us  [pack_call(): pl.pallas_call(functools.partial(pack_kernel, chunks, points_own, all_poi...]
    ppermute x1, waiting for transfers between devices: 21.7 us -> 7.73 us  [encoder(): mesh_far = lax.ppermute(mesh_latent, 'ch', across)]
    ppermute x1, waiting for transfers between devices: 0.01 us -> 12.4 us  [encoder(): low_own = lax.ppermute(low_half, 'lon', forward)]
    ppermute x1, waiting for transfers between devices: 10.9 us -> 0.01 us  [encoder(): bundle_far = lax.ppermute(bundle, ('lon', 'ch'), facing)]
    ppermute x0 -> x3, waiting for transfers between devices: none -> 7.48 us  [the longest x1 7.48 us: encoder(): message_far = lax.ppermute(message_weight, ('lon', 'ch'), facing)]
    ppermute x1, waiting for transfers between devices: 0.01 us -> 3.41 us  [encoder(): high_own = lax.ppermute(high_half, 'lon', backward)]
    ppermute x1, waiting for transfers between devices: 3.6 us -> 0.48 us  [encoder(): mesh_last = lax.ppermute(mesh_far, 'ch', swap)]
  transfers between devices with their start and end apart: 13 -> 16, of which waited for: 6 -> 8; matrix products, arithmetic and copies ran while one was open for 1% -> 1% of each run, Pallas kernels for 11% -> 21%
where the time goes in v4:
time: 112 us
  Pallas kernels  48.8 us (44%)
  waiting for transfers between devices  41.2 us (37%)
  starting transfers between devices  9.47 us (8%)
  blocking collectives  7.59 us (7%)
  other arithmetic  3.81 us (3%)
    pallas_call x2, Pallas kernels, block_call(): pl.pallas_call(functools.partial(block_kernel, outer, chunks, own_columns...  42.9 us
    ppermute x1, waiting for transfers between devices, encoder(): low_own = lax.ppermute(low_half, 'lon', forward)  12.4 us
    ppermute x1, waiting for transfers between devices, encoder(): mesh_far = lax.ppermute(mesh_latent, 'ch', across)  7.73 us
    psum x1, blocking collectives, encoder(): lax.psum((jnp.sum(node_share, axis=1, keepdims=True), jnp.sum(jnp.square(...  7.59 us
    ppermute x1, waiting for transfers between devices, encoder(): message_far = lax.ppermute(message_weight, ('lon', 'ch'), facing)  7.48 us
    ppermute x1, waiting for transfers between devices, encoder(): far = lax.ppermute(far.astype(bf16), 'ch', across).astype(f32)  7.13 us
    pallas_call x1, Pallas kernels, pack_call(): pl.pallas_call(functools.partial(pack_kernel, chunks, points_own, all_poi...  4.13 us
    ppermute x1, waiting for transfers between devices, encoder(): high_own = lax.ppermute(high_half, 'lon', backward)  3.41 us
  transfers between devices with their start and end apart: 16, of which 8 were waited for; matrix products, arithmetic and copies ran while one was open for 1% of the time, Pallas kernels for 21%

profile of v4, /device:TPU:6, one launch (start us, length us, event | category | flops | bytes accessed | tf_op | source)
XLA Modules:
  0.0 111.9 jit_solution(13080628600509201051)
XLA Ops:
  0.0 0.6 pad_add_fusion.place
  0.6 0.0 copy-start.10
  0.6 0.0 copy-start.2
  0.6 4.1 %pack.1 = (s32[44,128]{1,0:T(8,128)}, s32[44,128]{1,0:T(8,128)}, s32[11]{0:T(128)}, s32[11]{0:T(128)}, bf16[474,1280]{1,0:T(8,128)(2,1)}, /*index=5*/bf16[474,1280]{1,0:T(8,128)(2,1)}) custom-call(s32[2]{0:T(128)} %pad_add_fusion.place, s32[176,128]{1,0:T(8,128)} %bitcast.20, s32[176,128]{1,0:T(8,128)} %bitcast.21, bf16[474,28800]{1,0:T(8,128)(2,1)} %bitcast.13), custom_call_target="tpu_custom_call" | custom-call | tf_op jit(solution)/shard_map/pack/pallas_call | solution.py:361
  4.8 1.6 %collective-permute-start = (bf16[474,1280]{1,0:T(8,128)(2,1)}, bf16[474,1280]{1,0:T(8,128)(2,1)S(1)}, u32[]{:S(2)}, u32[]{:S(2)}) collective-permute-start(bf16[474,1280]{1,0:T(8,128)(2,1)} %get-tuple-element.21), channel_id=1, source_target_pairs={{0,4},{4,8},{8,12},{12,16},{16,20},{20,24},{24,28},{28,32},{32,36}... | collective-permute-start | bytes 3640328 | tf_op jit(solution)/shard_map/ppermute | solution.py:476
  6.3 0.5 collective-permute-start.2
  6.8 1.8 %weights.1.refs_10_.refs_14_ = bf16[1040,128]{1,0:T(8,128)(2,1)} custom-call(s32[2]{0:T(128)} %pad_add_fusion.place, bf16[4,128]{1,0:T(4,128)(2,1)} %feature_weight.1, f32[1,128]{1,0:T(1,128)} %bitcast.27, bf16[512,128]{1,0:T(8,128)(2,1)} %sender_weight.1, bf16[512,128]{1,0:T(8,128)(2,1)} %receiver_weight.1), custom_call_target="tpu_custom_call" | custom-call | tf_op jit(solution)/shard_map/weights/pallas_call | solution.py:347
  8.6 3.0 %collective-permute-start.5 = (bf16[1040,128]{1,0:T(8,128)(2,1)}, bf16[1040,128]{1,0:T(8,128)(2,1)S(1)}, u32[]{:S(2)}, u32[]{:S(2)}) collective-permute-start(bf16[1040,128]{1,0:T(8,128)(2,1)} %weights.1.refs_10_.refs_14_), channel_id=1, source_target_pairs={{0,18},{1,19},{2,16},{3,17},{4,22},{5,23},{6,20},{7,21},{8,26},{9,... | collective-permute-start | bytes 798728 | tf_op jit(solution)/shard_map/ppermute | solution.py:470
  11.7 0.0 copy-done.10
  11.7 0.2 collective-permute-start.11
  11.9 0.0 copy-done.2
  11.9 2.0 %collective-permute-start.8 = (bf16[640,128]{1,0:T(8,128)(2,1)S(1)}, bf16[640,128]{1,0:T(8,128)(2,1)S(1)}, u32[]{:S(2)}, u32[]{:S(2)}) collective-permute-start(bf16[640,128]{1,0:T(8,128)(2,1)S(1)} %copy-done.2), channel_id=1, source_target_pairs={{0,2},{1,3},{2,0},{3,1},{4,6},{5,7},{6,4},{7,5},{8,10},{9,11},{10,... | collective-permute-start | bytes 491528 | tf_op jit(solution)/shard_map/ppermute | solution.py:471
  13.9 7.5 %collective-permute-done.11.refs_24_ = bf16[128,512]{1,0:T(8,128)(2,1)S(1)} collective-permute-done((bf16[128,512]{1,0:T(8,128)(2,1)S(1)}, bf16[128,512]{1,0:T(8,128)(2,1)S(1)}, u32[]{:S(2)}, u32[]{:S(2)}) %collective-permute-start.11) | collective-permute-done | bytes 131104 | tf_op jit(solution)/shard_map/ppermute | solution.py:484
  21.3 0.0 copy-start.11
  21.3 0.0 collective-permute-start.7
  21.3 12.4 %collective-permute-done.refs_6_ = bf16[474,1280]{1,0:T(8,128)(2,1)S(1)} collective-permute-done((bf16[474,1280]{1,0:T(8,128)(2,1)}, bf16[474,1280]{1,0:T(8,128)(2,1)S(1)}, u32[]{:S(2)}, u32[]{:S(2)}) %collective-permute-start) | collective-permute-done | bytes 1213472 | tf_op jit(solution)/shard_map/ppermute | solution.py:476
  33.8 0.0 copy-start
  33.8 0.0 collective-permute-start.1
  33.8 3.4 %collective-permute-done.2.refs_8_ = bf16[474,1280]{1,0:T(8,128)(2,1)S(1)} collective-permute-done((bf16[474,1280]{1,0:T(8,128)(2,1)}, bf16[474,1280]{1,0:T(8,128)(2,1)S(1)}, u32[]{:S(2)}, u32[]{:S(2)}) %collective-permute-start.2) | collective-permute-done | bytes 1213472 | tf_op jit(solution)/shard_map/ppermute | solution.py:477
  37.2 0.0 copy-start.1
  37.2 0.0 collective-permute-start.3
  37.2 7.7 %collective-permute-done.8.refs_16_.refs_20_ = bf16[640,128]{1,0:T(8,128)(2,1)S(1)} collective-permute-done((bf16[640,128]{1,0:T(8,128)(2,1)S(1)}, bf16[640,128]{1,0:T(8,128)(2,1)S(1)}, u32[]{:S(2)}, u32[]{:S(2)}) %collective-permute-start.8) | collective-permute-done | bytes 163872 | tf_op jit(solution)/shard_map/ppermute | solution.py:471
  45.0 0.0 collective-permute-start.4
  45.0 0.0 collective-permute-done.5.refs_12_.refs_16_
  45.0 0.0 copy-start.4
  45.0 0.5 collective-permute-start.6
  45.5 0.0 collective-permute-done.7.refs_15_.refs_19_
  45.5 0.1 collective-permute-start.9
  45.6 1.1 %collective-permute-done.4.refs_11_.refs_15_ = bf16[1040,128]{1,0:T(8,128)(2,1)S(1)} collective-permute-done((bf16[1040,128]{1,0:T(8,128)(2,1)}, bf16[1040,128]{1,0:T(8,128)(2,1)S(1)}, u32[]{:S(2)}, u32[]{:S(2)}) %collective-permute-start.4) | collective-permute-done | bytes 266272 | tf_op jit(solution)/shard_map/ppermute | solution.py:480
  46.7 0.1 collective-permute-start.10
  46.8 0.5 collective-permute-done.9.refs_17_.refs_21_
  47.3 0.1 collective-permute-start.12
  47.5 0.0 collective-permute-done.6.refs_13_.refs_17_
  47.5 0.0 copy-done.7
  47.5 0.0 copy-done.4
  47.5 0.0 copy-done.8
  47.5 0.0 copy-done.5
  47.5 0.5 copy-done.9
  48.0 0.2 copy-done.6
  48.2 21.9 %block_inner.1 = (f32[640,512]{1,0:T(8,128)}, f32[640,128]{1,0:T(8,128)}) custom-call(s32[1]{0:T(128)} %bitcast.refs_0_, s32[5632]{0:T(1024)} %bitcast.22, s32[5632]{0:T(1024)} %bitcast.18, s32[11]{0:T(128)} %get-tuple-element.19.refs_3_, s32[11]{0:T(128)} %get-tuple-element.20.refs_4_, bf16[474,28800]{1,0:T(8,128)(2,1)} %bitcast.14, ...), custom_call_target="tpu_custom_call" | custom-call | flops 9596567552 | bytes 5767168 | tf_op jit(solution)/shard_map/block_inner/pallas_call | solution.py:389
  70.2 0.0 copy-done.11
  70.2 0.0 copy-done
  70.2 0.0 copy-done.1
  70.2 0.0 collective-permute-done.10.refs_23_
  70.2 0.0 collective-permute-done.12.refs_25_
  70.2 0.0 collective-permute-done.1.refs_7_
  70.2 0.0 collective-permute-done.3.refs_9_
  70.2 21.0 %block_outer.1 = (f32[640,128]{1,0:T(8,128)}, f32[640,128]{1,0:T(8,128)}, f32[640,128]{1,0:T(8,128)}, f32[640,128]{1,0:T(8,128)}) custom-call(s32[1]{0:T(128)} %bitcast.refs_0_, s32[5632]{0:T(1024)} %bitcast.23, s32[5632]{0:T(1024)} %bitcast.19, s32[11]{0:T(128)} %get-tuple-element.19.refs_3_, s32[11]{0:T(128)} %get-tuple-element.20.refs_4_, ...), custom_call_target="tpu_custom_call" | custom-call | flops 9596567552 | bytes 5767168 | tf_op jit(solution)/shard_map/block_outer/pallas_call | solution.py:389
  91.2 0.0 copy-start.3
  91.2 0.0 copy-start.12
  91.2 0.0 copy-start.13
  91.2 0.1 collective-permute-start.14
  91.3 0.5 collective-permute-start.13
  91.8 1.3 %collective-permute-done.14 = f32[640,128]{1,0:T(8,128)S(1)} collective-permute-done((f32[640,128]{1,0:T(8,128)}, f32[640,128]{1,0:T(8,128)S(1)}, u32[]{:S(2)}, u32[]{:S(2)}) %collective-permute-start.14) | collective-permute-done | bytes 327712 | tf_op jit(solution)/shard_map/ppermute | solution.py:509
  93.2 1.0 add_convert_fusion.1
  94.2 0.7 collective-permute-start.15
  94.9 0.0 collective-permute-done.13
  94.9 7.1 %collective-permute-done.15 = bf16[640,128]{1,0:T(8,128)(2,1)S(1)} collective-permute-done((bf16[640,128]{1,0:T(8,128)(2,1)S(1)}, bf16[640,128]{1,0:T(8,128)(2,1)S(1)}, u32[]{:S(2)}, u32[]{:S(2)}) %collective-permute-start.15) | collective-permute-done | bytes 163872 | tf_op jit(solution)/shard_map/ppermute | solution.py:510
  102.0 1.2 %fusion = (f32[640]{0:T(1024)S(1)}, f32[640]{0:T(1024)S(1)}, f32[640,128]{1,0:T(8,128)S(1)}) fusion(bf16[640,128]{1,0:T(8,128)(2,1)S(1)} %collective-permute-done.15, f32[640,128]{1,0:T(8,128)} %get-tuple-element.25, f32[640,128]{1,0:T(8,128)S(1)} %collective-permute-done.13), kind=kLoop, calls=%fused_computation.7 | loop fusion | flops 490240 | bytes 1152000 | tf_op jit(solution)/shard_map/reduce_sum | solution.py:514
  103.3 7.6 %all-reduce = (f32[640,1]{0,1:T(1,128)S(1)}, f32[640,1]{0,1:T(1,128)S(1)}) all-reduce(f32[640,1]{0,1:T(1,128)S(1)} %broadcast_in_dim.24, f32[640,1]{0,1:T(1,128)S(1)} %broadcast_in_dim.25), channel_id=1, replica_groups=mesh['lon'=32,'ch'=4] {'ch'}, use_global_device_ids=true, to_apply=%region_1.0 | all-reduce | flops 1280 | bytes 10240 | tf_op jit(solution)/shard_map/psum | solution.py:512
  110.9 0.0 copy-done.3
  110.9 0.0 copy-done.12
  110.9 0.0 copy-done.13
  110.9 0.9 add_convert_fusion
  (8 shorter events, 0.0 us)
Async XLA Ops:
  0.6 11.0 %copy-start.10 = (bf16[128,512]{1,0:T(8,128)(2,1)S(1)}, bf16[128,512]{1,0:T(8,128)(2,1)}, u32[]{:S(2)}) copy-start(bf16[128,512]{1,0:T(8,128)(2,1)} %refs_22_.1) | copy-start | bytes 393220
  0.6 11.3 %copy-start.2 = (bf16[640,128]{1,0:T(8,128)(2,1)S(1)}, bf16[640,128]{1,0:T(8,128)(2,1)}, u32[]{:S(2)}) copy-start(bf16[640,128]{1,0:T(8,128)(2,1)} %refs_18_.1) | copy-start | bytes 491524
  4.8 29.0 %collective-permute-start = (bf16[474,1280]{1,0:T(8,128)(2,1)}, bf16[474,1280]{1,0:T(8,128)(2,1)S(1)}, u32[]{:S(2)}, u32[]{:S(2)}) collective-permute-start(bf16[474,1280]{1,0:T(8,128)(2,1)} %get-tuple-element.21), channel_id=1, source_target_pairs={{0,4},{4,8},{8,12},{12,16},{16,20},{20,24},{24,28},{28,32},{32,36}... | collective-permute-start | bytes 3640328 | tf_op jit(solution)/shard_map/ppermute | solution.py:476
  6.3 30.9 %collective-permute-start.2 = (bf16[474,1280]{1,0:T(8,128)(2,1)}, bf16[474,1280]{1,0:T(8,128)(2,1)S(1)}, u32[]{:S(2)}, u32[]{:S(2)}) collective-permute-start(bf16[474,1280]{1,0:T(8,128)(2,1)} %get-tuple-element.22), channel_id=1, source_target_pairs={{4,0},{8,4},{12,8},{16,12},{20,16},{24,20},{28,24},{32,28},{36,32}... | collective-permute-start | bytes 3640328 | tf_op jit(solution)/shard_map/ppermute | solution.py:477
  8.6 36.3 %collective-permute-start.5 = (bf16[1040,128]{1,0:T(8,128)(2,1)}, bf16[1040,128]{1,0:T(8,128)(2,1)S(1)}, u32[]{:S(2)}, u32[]{:S(2)}) collective-permute-start(bf16[1040,128]{1,0:T(8,128)(2,1)} %weights.1.refs_10_.refs_14_), channel_id=1, source_target_pairs={{0,18},{1,19},{2,16},{3,17},{4,22},{5,23},{6,20},{7,21},{8,26},{9,... | collective-permute-start | bytes 798728 | tf_op jit(solution)/shard_map/ppermute | solution.py:470
  11.7 9.7 %collective-permute-start.11 = (bf16[128,512]{1,0:T(8,128)(2,1)S(1)}, bf16[128,512]{1,0:T(8,128)(2,1)S(1)}, u32[]{:S(2)}, u32[]{:S(2)}) collective-permute-start(bf16[128,512]{1,0:T(8,128)(2,1)S(1)} %copy-done.10), channel_id=1, source_target_pairs={{0,18},{1,19},{2,16},{3,17},{4,22},{5,23},{6,20},{7,21},{8,26},{9,... | collective-permute-start | bytes 393224 | tf_op jit(solution)/shard_map/ppermute | solution.py:484
  11.9 33.1 %collective-permute-start.8 = (bf16[640,128]{1,0:T(8,128)(2,1)S(1)}, bf16[640,128]{1,0:T(8,128)(2,1)S(1)}, u32[]{:S(2)}, u32[]{:S(2)}) collective-permute-start(bf16[640,128]{1,0:T(8,128)(2,1)S(1)} %copy-done.2), channel_id=1, source_target_pairs={{0,2},{1,3},{2,0},{3,1},{4,6},{5,7},{6,4},{7,5},{8,10},{9,11},{10,... | collective-permute-start | bytes 491528 | tf_op jit(solution)/shard_map/ppermute | solution.py:471
  21.3 48.8 %copy-start.11 = (bf16[128,512]{1,0:T(8,128)(2,1)}, bf16[128,512]{1,0:T(8,128)(2,1)S(1)}, u32[]{:S(2)}) copy-start(bf16[128,512]{1,0:T(8,128)(2,1)S(1)} %collective-permute-done.11.refs_24_) | copy-start | bytes 393220
  21.3 24.1 %collective-permute-start.7 = (bf16[640,128]{1,0:T(8,128)(2,1)S(1)}, bf16[640,128]{1,0:T(8,128)(2,1)S(1)}, u32[]{:S(2)}, u32[]{:S(2)}) collective-permute-start(bf16[640,128]{1,0:T(8,128)(2,1)S(1)} %copy-done.2), channel_id=1, source_target_pairs={{0,1},{1,0},{2,3},{3,2},{4,5},{5,4},{6,7},{7,6},{8,9},{9,8},{10,11... | collective-permute-start | bytes 491528 | tf_op jit(solution)/shard_map/ppermute | solution.py:482
  33.8 36.4 %copy-start = (bf16[474,1280]{1,0:T(8,128)(2,1)}, bf16[474,1280]{1,0:T(8,128)(2,1)S(1)}, u32[]{:S(2)}) copy-start(bf16[474,1280]{1,0:T(8,128)(2,1)S(1)} %collective-permute-done.refs_6_) | copy-start | bytes 3640324
  33.8 36.4 %collective-permute-start.1 = (bf16[474,1280]{1,0:T(8,128)(2,1)S(1)}, bf16[474,1280]{1,0:T(8,128)(2,1)}, u32[]{:S(2)}, u32[]{:S(2)}) collective-permute-start(bf16[474,1280]{1,0:T(8,128)(2,1)S(1)} %collective-permute-done.refs_6_), channel_id=1, source_target_pairs={{0,1},{1,0},{2,3},{3,2},{4,5},{5,4},{6,7},{7,6},{8,9},{9,8},{10,11... | collective-permute-start | bytes 3640328 | tf_op jit(solution)/shard_map/ppermute | solution.py:478
  37.2 33.0 %copy-start.1 = (bf16[474,1280]{1,0:T(8,128)(2,1)}, bf16[474,1280]{1,0:T(8,128)(2,1)S(1)}, u32[]{:S(2)}) copy-start(bf16[474,1280]{1,0:T(8,128)(2,1)S(1)} %collective-permute-done.2.refs_8_) | copy-start | bytes 3640324
  37.2 33.0 %collective-permute-start.3 = (bf16[474,1280]{1,0:T(8,128)(2,1)S(1)}, bf16[474,1280]{1,0:T(8,128)(2,1)}, u32[]{:S(2)}, u32[]{:S(2)}) collective-permute-start(bf16[474,1280]{1,0:T(8,128)(2,1)S(1)} %collective-permute-done.2.refs_8_), channel_id=1, source_target_pairs={{0,1},{1,0},{2,3},{3,2},{4,5},{5,4},{6,7},{7,6},{8,9},{9,8},{10,11... | collective-permute-start | bytes 3640328 | tf_op jit(solution)/shard_map/ppermute | solution.py:479
  45.0 2.5 %copy-start.7 = (bf16[640,128]{1,0:T(8,128)(2,1)}, bf16[640,128]{1,0:T(8,128)(2,1)S(1)}, u32[]{:S(2)}) copy-start(bf16[640,128]{1,0:T(8,128)(2,1)S(1)} %collective-permute-done.8.refs_16_.refs_20_) | copy-start | bytes 491524
  45.0 1.8 %collective-permute-start.4 = (bf16[1040,128]{1,0:T(8,128)(2,1)}, bf16[1040,128]{1,0:T(8,128)(2,1)S(1)}, u32[]{:S(2)}, u32[]{:S(2)}) collective-permute-start(bf16[1040,128]{1,0:T(8,128)(2,1)} %weights.1.refs_10_.refs_14_), channel_id=1, source_target_pairs={{0,1},{1,0},{2,3},{3,2},{4,5},{5,4},{6,7},{7,6},{8,9},{9,8},{10,11... | collective-permute-start | bytes 798728 | tf_op jit(solution)/shard_map/ppermute | solution.py:480
  45.0 2.5 %copy-start.4 = (bf16[1040,128]{1,0:T(8,128)(2,1)}, bf16[1040,128]{1,0:T(8,128)(2,1)S(1)}, u32[]{:S(2)}) copy-start(bf16[1040,128]{1,0:T(8,128)(2,1)S(1)} %collective-permute-done.5.refs_12_.refs_16_) | copy-start | bytes 798724
  45.0 2.5 %collective-permute-start.6 = (bf16[1040,128]{1,0:T(8,128)(2,1)S(1)}, bf16[1040,128]{1,0:T(8,128)(2,1)S(1)}, u32[]{:S(2)}, u32[]{:S(2)}) collective-permute-start(bf16[1040,128]{1,0:T(8,128)(2,1)S(1)} %collective-permute-done.5.refs_12_.refs_16_), channel_id=1, source_target_pairs={{0,1},{1,0},{2,3},{3,2},{4,5},{5,4},{6,7},{7,6},{8,9},{9,8},{10,11... | collective-permute-start | bytes 798728 | tf_op jit(solution)/shard_map/ppermute | solution.py:481
  45.5 2.0 %copy-start.8 = (bf16[640,128]{1,0:T(8,128)(2,1)}, bf16[640,128]{1,0:T(8,128)(2,1)S(1)}, u32[]{:S(2)}) copy-start(bf16[640,128]{1,0:T(8,128)(2,1)S(1)} %collective-permute-done.7.refs_15_.refs_19_) | copy-start | bytes 491524
  45.5 1.8 %collective-permute-start.9 = (bf16[640,128]{1,0:T(8,128)(2,1)S(1)}, bf16[640,128]{1,0:T(8,128)(2,1)S(1)}, u32[]{:S(2)}, u32[]{:S(2)}) collective-permute-start(bf16[640,128]{1,0:T(8,128)(2,1)S(1)} %collective-permute-done.8.refs_16_.refs_20_), channel_id=1, source_target_pairs={{0,1},{1,0},{2,3},{3,2},{4,5},{5,4},{6,7},{7,6},{8,9},{9,8},{10,11... | collective-permute-start | bytes 491528 | tf_op jit(solution)/shard_map/ppermute | solution.py:483
  46.7 0.8 copy-start.5
  46.7 23.5 %collective-permute-start.10 = (bf16[128,512]{1,0:T(8,128)(2,1)S(1)}, bf16[128,512]{1,0:T(8,128)(2,1)}, u32[]{:S(2)}, u32[]{:S(2)}) collective-permute-start(bf16[128,512]{1,0:T(8,128)(2,1)S(1)} %copy-done.10), channel_id=1, source_target_pairs={{0,1},{1,0},{2,3},{3,2},{4,5},{5,4},{6,7},{7,6},{8,9},{9,8},{10,11... | collective-permute-start | bytes 393224 | tf_op jit(solution)/shard_map/ppermute | solution.py:485
  47.3 0.7 copy-start.9
  47.3 22.9 %collective-permute-start.12 = (bf16[128,512]{1,0:T(8,128)(2,1)S(1)}, bf16[128,512]{1,0:T(8,128)(2,1)}, u32[]{:S(2)}, u32[]{:S(2)}) collective-permute-start(bf16[128,512]{1,0:T(8,128)(2,1)S(1)} %collective-permute-done.11.refs_24_), channel_id=1, source_target_pairs={{0,1},{1,0},{2,3},{3,2},{4,5},{5,4},{6,7},{7,6},{8,9},{9,8},{10,11... | collective-permute-start | bytes 393224 | tf_op jit(solution)/shard_map/ppermute | solution.py:486
  47.5 0.7 copy-start.6
  91.2 19.7 %copy-start.3 = (bf16[640,128]{1,0:T(8,128)(2,1)S(1)}, bf16[640,128]{1,0:T(8,128)(2,1)}, u32[]{:S(2)}) copy-start(bf16[640,128]{1,0:T(8,128)(2,1)} %refs_18_.1) | copy-start | bytes 491524
  91.2 19.7 %copy-start.12 = (f32[128]{0:T(128)S(1)}, f32[128]{0:T(128)}, u32[]{:S(2)}) copy-start(f32[128]{0:T(128)} %param.29) | copy-start | bytes 1540
  91.2 19.7 %copy-start.13 = (f32[128]{0:T(128)S(1)}, f32[128]{0:T(128)}, u32[]{:S(2)}) copy-start(f32[128]{0:T(128)} %param.28) | copy-start | bytes 1540
  91.2 1.9 %collective-permute-start.14 = (f32[640,128]{1,0:T(8,128)}, f32[640,128]{1,0:T(8,128)S(1)}, u32[]{:S(2)}, u32[]{:S(2)}) collective-permute-start(f32[640,128]{1,0:T(8,128)} %get-tuple-element.28), channel_id=1, source_target_pairs={{0,1},{1,0},{2,3},{3,2},{4,5},{5,4},{6,7},{7,6},{8,9},{9,8},{10,11... | collective-permute-start | bytes 983048 | tf_op jit(solution)/shard_map/ppermute | solution.py:509
  91.3 3.6 %collective-permute-start.13 = (f32[640,128]{1,0:T(8,128)}, f32[640,128]{1,0:T(8,128)S(1)}, u32[]{:S(2)}, u32[]{:S(2)}) collective-permute-start(f32[640,128]{1,0:T(8,128)} %get-tuple-element.26), channel_id=1, source_target_pairs={{0,1},{1,0},{2,3},{3,2},{4,5},{5,4},{6,7},{7,6},{8,9},{9,8},{10,11... | collective-permute-start | bytes 983048 | tf_op jit(solution)/shard_map/ppermute | solution.py:511
  94.2 7.8 %collective-permute-start.15 = (bf16[640,128]{1,0:T(8,128)(2,1)S(1)}, bf16[640,128]{1,0:T(8,128)(2,1)S(1)}, u32[]{:S(2)}, u32[]{:S(2)}) collective-permute-start(bf16[640,128]{1,0:T(8,128)(2,1)S(1)} %add_convert_fusion.1), channel_id=1, source_target_pairs={{0,2},{1,3},{2,0},{3,1},{4,6},{5,7},{6,4},{7,5},{8,10},{9,11},{10,... | collective-permute-start | bytes 491528 | tf_op jit(solution)/shard_map/ppermute | solution.py:510
